TPU v7x, 32 devices: a 4x4x1 block of a 4x4x8 slice. The times are simulated.
32 devices in a mesh: sweep: 1 (over z), data: 4 (over y), ent: 8 (over x, core).
Axes of the slice: x: 4, y: 4, z: 1, core: 2. Of those that a mesh axis runs over, the one named last changes fastest.
The devices are a block of a 4x4x8 slice.
Arguments:
- ent_table: float32 [32768, 400], P(('sweep', 'ent'))
- ent_state: float32 [32768], P(('sweep', 'ent'))
- rel_table: float32 [107, 400], P('sweep')
- head_idx: int32 [8, 8, 8192], P(('sweep', 'ent'), None, 'data')
- tail_idx: int32 [8, 8, 8192], P(('sweep', 'ent'), None, 'data')
- rel_idx: int32 [8, 8, 8192], P(('sweep', 'ent'), None, 'data')
- edge_mask: int32 [8, 8, 8192], P(('sweep', 'ent'), None, 'data')
- neg_idx: int32 [8, 8, 1024], P(('sweep', 'ent'))
Outputs:
- output 1: float32 [32768, 400], P(('sweep', 'ent'))
- output 2: float32 [32768], P(('sweep', 'ent'))
- output 3: float32 [107, 400], P('sweep')
- output 4: float32 [8, 8], P(('sweep', 'ent'))
All inputs are finite; a program needn't handle non-finite values.
Results may differ from a plain program's by a relative error of at most 0.001.
Values are sent between devices in bfloat16 or wider.
A program may use at most 768 MiB of HBM per device.

v0:
```python
import functools

import jax
import jax.numpy as jnp
from jax import lax
from jax.experimental import pallas as pl
from jax.experimental.pallas import tpu as pltpu
from jax.sharding import PartitionSpec as P

LR_SCALE = 0.2
EPSILON = 1e-8
LANES = 128
HALF = 64
LEFT = 8
BLOCK = 256
CHUNK = 128
UNROLL = 64
ROLLED = 32
TOGETHER = 4
LAG = 3
PARTS = 4
REL_HOPS = 6
STRIP = 32
REL_PAD = 128
TILES = range(4)
CORES = range(2)
ROW_COL, ROW_ROW, COL_COL = (((1,), (0,)), ((1,), (1,)), ((0,), (0,)))
F32 = jnp.float32
BF16 = jnp.bfloat16
VMEM_LIMIT = 60 * 2**20


def roll(x, by):
    return pltpu.roll(x, by, 1)


def beside(parts):
    return jnp.concatenate(parts, axis=1)


def below(parts):
    return jnp.concatenate(parts, axis=0)


def lanes(shape):
    return lax.broadcasted_iota(jnp.int32, shape, 1)


def sublanes(shape):
    return lax.broadcasted_iota(jnp.int32, shape, 0)


def row_sum(x):
    return jnp.sum(x, axis=1, keepdims=True)


def wire_rows(rows):
    return 3 * rows + rows // LEFT


def columns_to_tiles(x):
    half = x.shape[0] // 2
    a, c, d = slice(0, LANES), slice(LANES, LANES + HALF), slice(LANES + HALF, half)
    re, im = x[:half], x[half:]
    zero = jnp.zeros((HALF - LEFT, x.shape[1]), x.dtype)
    return [t.T for t in (re[a], im[a], below([re[c], im[c]]), below([re[d], zero, im[d], zero]))]


def tiles_to_columns(tiles):
    a, b, c, d = (t.T for t in tiles)
    high = slice(HALF, HALF + LEFT)
    return below([a, c[:HALF], d[:LEFT], b, c[HALF:], d[high]])


def each_row(count, body):
    for u in range(count):
        body(u)


def band(n, size):
    return slice(n * size, (n + 1) * size)


def where_here():
    y, ent = lax.axis_index('data'), lax.axis_index('ent')
    return y, ent // 2, ent % 2, y // 2, y % 2


def fold_last(tile):
    n = tile.shape[0] // LEFT
    out = tile[:n]
    for k in range(1, LEFT):
        out = out + roll(tile[band(k, n)], LEFT * k)
    return out


def unfold_last(packed):
    keep = lanes(packed.shape) % HALF < LEFT
    return [jnp.where(keep, packed if k == 0 else roll(packed, LANES - LEFT * k), 0.0) for k in range(LEFT)]


def tiles_of(x):
    return [x[:, band(t, LANES)] for t in TILES]


def times(x, y):
    out = [x[0] * y[0] - x[1] * y[1], x[0] * y[1] + x[1] * y[0]]
    for a, b in zip(x[2:], y[2:]):
        low = lanes(a.shape) < HALF
        a_swap, b_swap = roll(a, HALF), roll(b, HALF)
        out.append(jnp.where(low, a * b - a_swap * b_swap, a_swap * b + a * b_swap))
    return out


def times_conj(x, y):
    out = [x[0] * y[0] + x[1] * y[1], x[1] * y[0] - x[0] * y[1]]
    for a, b in zip(x[2:], y[2:]):
        low = lanes(a.shape) < HALF
        a_swap, b_swap = roll(a, HALF), roll(b, HALF)
        out.append(jnp.where(low, a * b + a_swap * b_swap, a * b_swap - a_swap * b))
    return out


def tiles_at(ref, row, rows):
    block = ref[pl.ds(row * 4, rows * 4), :].reshape(rows // 8, 32, LANES)
    return [block[:, 8 * t:8 * t + 8].reshape(rows, LANES) for t in TILES]


def stack_tiles(tiles):
    rows = tiles[0].shape[0]
    return beside([t.reshape(rows // 8, 8, LANES) for t in tiles]).reshape(rows * 4, LANES)


def row_at(address):
    return pl.ds(address, 4, stride=8)


def row_address(row):
    return (row >> 3 << 5) | (row & 7)


def in_three(x):
    pieces = []
    for _ in range(3):
        piece = x.astype(BF16)
        pieces.append(piece)
        x = x - piece.astype(F32)
    return pieces


def dot(x, y, dims):
    return lax.dot_general(x, y, (dims, ((), ())), preferred_element_type=F32)


def bucket_kernel(cfg, edges_hbm, count_ref, negs_hbm, rel_ids_hbm, ent_hbm, rel_ref, table_hbm, tail_hbm, head_hbm, rel_out,
                  tail_rows, head_next, tail_next, head_buf, tail_buf, gh_last, gt_last, rel_buf, query_buf, pos_buf, score_buf, d_neg_buf, grad_buf, piece_buf,
                  neg_rows, neg_grad, rel_three, tail_acc0, tail_acc1, head_acc0, head_acc1, rel_acc, loss_acc,
                  edge_ref, neg_ref, rel_id_ref, ent_ref, table_ref, tail_out, head_out, sems, table_sems, tail_sems):
    step, tail_bits = cfg
    chunk = CHUNK
    part = chunk // LEFT
    tail_acc, head_acc = (tail_acc0, tail_acc1), (head_acc0, head_acc1)
    count = count_ref[step, 0]
    negs = neg_ref.shape[0]
    loads = [
        pltpu.make_async_copy(negs_hbm.at[step, 0], neg_ref, sems.at[0]),
        pltpu.make_async_copy(rel_ids_hbm.at[step], rel_id_ref, sems.at[2]),
        pltpu.make_async_copy(ent_hbm, ent_ref, sems.at[3]),
    ]
    parts = table_sems.shape[0]
    size = table_ref.shape[0] // parts
    tables = [pltpu.make_async_copy(table_hbm.at[band(n, size)], table_ref.at[band(n, size)], table_sems.at[n]) for n in range(parts)]
    blocks = pl.cdiv(count, BLOCK)

    def edge_pieces(act):
        def one(n, carry):
            span = pl.ds(pl.multiple_of(n * 2 * BLOCK, 2 * BLOCK), 2 * BLOCK)
            act(pltpu.make_async_copy(edges_hbm.at[step, 0, span], edge_ref.at[span], sems.at[1]))
            return carry

        lax.fori_loop(0, (blocks + 3) // 2, one, 0)

    edge_pieces(lambda copy: copy.start())
    for load in loads + tables:
        load.start()

    def head_of(e):
        return row_at(e >> tail_bits)

    def tail_of(e):
        return row_at(e & (2**tail_bits - 1))

    def clear(accs, n, carry):
        for acc in accs:
            acc[pl.ds(pl.multiple_of(n * chunk * 4, chunk * 4), chunk * 4), :] = jnp.zeros((chunk * 4, LANES), F32)
        return carry

    lax.fori_loop(0, table_ref.shape[0], functools.partial(clear, tail_acc), 0)
    lax.fori_loop(0, head_out.shape[0], functools.partial(clear, head_acc), 0)
    neg_grad[...] = jnp.zeros_like(neg_grad)
    gh_last[...] = jnp.zeros_like(gh_last)
    gt_last[...] = jnp.zeros_like(gt_last)
    rel_acc[...] = jnp.zeros_like(rel_acc)
    loss_acc[...] = jnp.zeros_like(loss_acc)
    for n, piece in enumerate(in_three(rel_ref[...])):
        rel_three[band(n, REL_PAD), :] = piece
    for load in loads:
        load.wait()
    edge_pieces(lambda copy: copy.wait())

    def widen(i, carry):
        for n in (i * TOGETHER + k for k in range(TOGETHER)):
            tiles = [table_ref[n, band(t, chunk), :].astype(F32) for t in TILES[:-1]]
            tiles.append(below(unfold_last(table_ref[n, 3 * chunk:, :].astype(F32))))
            tail_rows[pl.ds(pl.multiple_of(n * chunk * 4, chunk * 4), chunk * 4), :] = stack_tiles(tiles)
        return carry

    for n, load in enumerate(tables):
        load.wait()
        lax.fori_loop(n * size // TOGETHER, (n + 1) * size // TOGETHER, widen, 0)

    def take_negs(n, carry):
        base = pl.multiple_of(n * UNROLL, UNROLL)

        def take(u):
            head_buf[row_at(row_address(u)), :] = tail_rows[row_at(neg_ref[base + u]), :]

        each_row(UNROLL, take)
        for t, tile in enumerate(tiles_at(head_buf, 0, UNROLL)):
            neg_rows[pl.ds(base, UNROLL), band(t, LANES)] = tile.astype(BF16)
        return carry

    lax.fori_loop(0, negs // UNROLL, take_negs, 0)

    def take_edges(base, row=0):
        def take(u):
            e = edge_ref[base + u]
            place = row_at(row * 4 + row_address(u))
            head_next[place, :] = ent_ref[head_of(e), :]
            tail_next[place, :] = tail_rows[tail_of(e), :]

        return take

    def put_edges(base, row=0):
        def put(pair):
            for lane in range(2):
                u = 2 * pair + lane
                e = edge_ref[base + u]
                place = row_at(row * 4 + row_address(u))
                head_acc[lane][head_of(e), :] += gh_last[place, :]
                tail_acc[lane][tail_of(e), :] += gt_last[place, :]

        return put


    def take_first(n, carry):
        row = pl.multiple_of(n * ROLLED, ROLLED)
        each_row(ROLLED, take_edges(BLOCK + row, row))
        return carry

    lax.fori_loop(0, BLOCK // ROLLED, take_first, 0)
    spans = [slice(r, r + STRIP) for r in range(0, BLOCK, STRIP)]

    def block(n, carry):
        base = pl.multiple_of(n * BLOCK, BLOCK)
        hot = sublanes((REL_PAD, BLOCK)) == rel_id_ref[:, pl.ds(base, BLOCK)]
        hot = jnp.where(hot, 1.0, 0.0).astype(BF16)
        rel_buf[...] = dot(below([hot] * 3), rel_three[...], COL_COL)
        for span in spans:
            head, tail, rel = tiles_at(head_next, span.start, STRIP), tiles_at(tail_next, span.start, STRIP), tiles_of(rel_buf[span, :])
            wide = slice(4 * span.start, 4 * span.stop)
            head_buf[wide, :], tail_buf[wide, :] = stack_tiles(head), stack_tiles(tail)
            total = None
            for t, q in enumerate(times(head, rel)):
                q = q.astype(BF16)
                query_buf[span, band(t, LANES)] = q
                product = q.astype(F32) * tail[t]
                total = product if total is None else total + product
            pos_buf[span, :] = row_sum(total)
        each_row(BLOCK, take_edges(base + 2 * BLOCK))
        each_row(BLOCK // 2, put_edges(base))
        score_buf[...] = dot(query_buf[...], neg_rows[...], ROW_ROW)
        for span in spans:
            weight = jnp.where(sublanes((STRIP, 1)) + (base + span.start) < count, 1.0, 0.0)
            score, pos = score_buf[span, :], pos_buf[span, :]
            top = jnp.maximum(jnp.max(score, axis=1, keepdims=True), pos)
            pos_exp = jnp.exp(pos - top)
            neg_exp = jnp.exp(score - top)
            total = pos_exp + row_sum(neg_exp)
            loss_acc[...] += jnp.sum(weight * (top + jnp.log(total) - pos), axis=0, keepdims=True)
            pos_buf[span, :] = weight * (pos_exp / total - 1.0)
            d_neg_buf[span, :] = ((weight / total) * neg_exp).astype(BF16)
        grad_buf[...] = dot(d_neg_buf[...], neg_rows[...], ROW_COL)
        neg_grad[...] += dot(d_neg_buf[...], query_buf[...], COL_COL)
        for span in spans:
            wide = slice(4 * span.start, 4 * span.stop)
            d_pos = pos_buf[span, :]
            tail, rel = tiles_at(tail_buf, span.start, STRIP), tiles_of(rel_buf[span, :])
            grad_q = [d_pos * x + y for x, y in zip(tail, tiles_of(grad_buf[span, :]))]
            gt_last[wide, :] = stack_tiles([d_pos * q.astype(F32) for q in tiles_of(query_buf[span, :])])
            gh_last[wide, :] = stack_tiles(times_conj(grad_q, rel))
            for t, grad in enumerate(times_conj(grad_q, tiles_at(head_buf, span.start, STRIP))):
                for k, piece in enumerate(in_three(grad)):
                    piece_buf[k * BLOCK + span.start:k * BLOCK + span.stop, band(t, LANES)] = piece
        rel_acc[...] += dot(beside([hot] * 3), piece_buf[...], ROW_COL)
        return carry

    lax.fori_loop(0, blocks, block, 0)

    def put_last(n, carry):
        row = pl.multiple_of(n * ROLLED, ROLLED)
        each_row(ROLLED // 2, put_edges(blocks * BLOCK + row, row))
        return carry

    lax.fori_loop(0, BLOCK // ROLLED, put_last, 0)

    def put_negs(n, carry):
        base = pl.multiple_of(n * UNROLL, UNROLL)
        gt_last[:4 * UNROLL, :] = stack_tiles(tiles_of(neg_grad[pl.ds(base, UNROLL), :]))

        def put(pair):
            for lane in range(2):
                u = 2 * pair + lane
                tail_acc[lane][row_at(neg_ref[base + u]), :] += gt_last[row_at(row_address(u)), :]

        each_row(UNROLL // 2, put)
        return carry

    lax.fori_loop(0, negs // UNROLL, put_negs, 0)

    def emit(out_ref, acc, i, carry):
        for n in (i * TOGETHER + k for k in range(TOGETHER)):
            base = pl.multiple_of(n * chunk, chunk)
            tiles = [a + b for a, b in zip(tiles_at(acc[0], base, chunk), tiles_at(acc[1], base, chunk))]
            for t in TILES[:-1]:
                out_ref[n, band(t, chunk), :] = tiles[t]
            out_ref[n, 3 * chunk:, :] = fold_last(tiles[3])
        return carry

    stores = []
    for n in range(tail_sems.shape[0]):
        out, dst, acc, span = (head_out, head_hbm, head_acc, range(head_out.shape[0])) if n == parts else (tail_out, tail_hbm, tail_acc, range(n * size, (n + 1) * size))
        lax.fori_loop(span.start // TOGETHER, span.stop // TOGETHER, functools.partial(emit, out, acc), 0)
        part_of = pl.ds(span.start, len(span))
        stores.append(pltpu.make_async_copy(out.at[part_of], dst.at[part_of], tail_sems.at[n]))
        stores[-1].start()
    _, x, _, top, _ = where_here()
    group = 2 * x + top
    row = sublanes((REL_PAD, LANES))
    lane = lanes((REL_PAD, LANES))
    loss = jnp.where(lane == group, loss_acc[...], 0.0)
    for t in TILES[:-1]:
        rows = rel_acc[:, band(t, LANES)]
        rel_out[band(t, REL_PAD), :] = jnp.where(row == REL_PAD - 1, loss, rows) if t == 0 else rows
    rel_out[3 * REL_PAD:, :] = fold_last(rel_acc[:, 3 * LANES:])
    for store in stores:
        store.wait()


def dma_sems(n):
    return pltpu.SemaphoreType.DMA((n,))


def bucket_call(step, tail_bits, edges, counts, negs, rel_ids, ent, rel, table):
    smem, vmem, hbm = (pl.BlockSpec(memory_space=m) for m in (pltpu.SMEM, pltpu.VMEM, pl.ANY))
    rows, neg_count, chunks = ent.shape[0] // 4, negs.shape[-1], table.shape[0]
    width = 4 * LANES
    wire = wire_rows(CHUNK)
    block = pltpu.VMEM((BLOCK * 4, LANES), F32)
    table_rows = pltpu.VMEM((chunks * CHUNK * 4, LANES), F32)
    head_rows = pltpu.VMEM((rows * 4, LANES), F32)
    return pl.pallas_call(
        functools.partial(bucket_kernel, (step, tail_bits)),
        out_shape=(
            jax.ShapeDtypeStruct((chunks, wire, LANES), F32),
            jax.ShapeDtypeStruct((rows // CHUNK, wire, LANES), F32),
            jax.ShapeDtypeStruct((wire_rows(REL_PAD), LANES), F32),
        ),
        in_specs=[hbm, smem, hbm, hbm, hbm, vmem, hbm],
        out_specs=(hbm, hbm, vmem),
        scratch_shapes=[
            table_rows, *[block] * 6, pltpu.VMEM((BLOCK, width), F32), pltpu.VMEM((BLOCK, width), BF16), pltpu.VMEM((BLOCK, 1), F32),
            pltpu.VMEM((BLOCK, neg_count), F32), pltpu.VMEM((BLOCK, neg_count), BF16), pltpu.VMEM((BLOCK, width), F32), pltpu.VMEM((3 * BLOCK, width), BF16),
            pltpu.VMEM((neg_count, width), BF16), pltpu.VMEM((neg_count, width), F32), pltpu.VMEM((3 * REL_PAD, width), BF16),
            table_rows, table_rows, head_rows, head_rows,
            pltpu.VMEM((REL_PAD, width), F32), pltpu.VMEM((1, 1), F32),
            pltpu.SMEM((edges.shape[-1],), jnp.int32), pltpu.SMEM((neg_count,), jnp.int32), pltpu.VMEM(rel_ids.shape[1:], jnp.int32),
            pltpu.VMEM(ent.shape, F32), pltpu.VMEM(table.shape, BF16), pltpu.VMEM((chunks, wire, LANES), F32), pltpu.VMEM((rows // CHUNK, wire, LANES), F32),
            dma_sems(4), dma_sems(PARTS), dma_sems(PARTS + 1),
        ],
        compiler_params=pltpu.CompilerParams(vmem_limit_bytes=VMEM_LIMIT),
        name='bucket',
    )(edges, counts, negs, rel_ids, ent, rel, table)


def entry(peers):
    barrier = pltpu.get_barrier_semaphore()
    for peer in peers:
        pl.semaphore_signal(barrier, inc=1, device_id=peer, device_id_type=pl.DeviceIdType.MESH)
    pl.semaphore_wait(barrier, len(peers))


def remote(src, dst, send, recv, peer):
    return pltpu.make_async_remote_copy(src_ref=src, dst_ref=dst, send_sem=send, recv_sem=recv, device_id=peer, device_id_type=pl.DeviceIdType.MESH)


def adagrad(rows, state, grad, mean_of, learn_rate):
    square = grad[0] * grad[0] + grad[1] * grad[1] + grad[2] * grad[2] + grad[3] * grad[3]
    state = state + row_sum(square) / mean_of
    root = jnp.sqrt(state + EPSILON)
    return [r - learn_rate * (g / root) for r, g in zip(rows, grad)], state


def exchange_kernel(cfg, tail_ref, head_hbm, rel_grad_ref, ent_hbm, state_ref, rel_ref, rel_state_ref, *refs):
    step, groups, chunks, emb_width, last = cfg
    if last:
        ent_wire, rel_out, loss_out, *refs = refs
    else:
        ent_out, state_out, rel_out, rel_state_out, loss_out, table_hbm, *refs, table, store_sem = refs
    (own, from_core, from_y, from_group, rel_sum, rel_from, send_buf,
     own_sem, core_send, core_recv, y_send, y_recv, group_send, group_recv, rel_send, rel_recv, out_send, out_recv, head_ref, ent_ref, row_sem) = refs
    learn_rate = LR_SCALE * emb_width ** -0.25
    chunk = CHUNK
    y, x, core, top, bot = where_here()
    mine = 2 * x + top
    x_size = groups // 2

    def place(group, low, c):
        return {'data': 2 * (group % 2) + low, 'ent': 2 * (group // 2) + c}

    def at(dy, dx, c):
        return {'data': dy, 'ent': 2 * dx + c}

    def slot_of(low, c, k):
        return (low * 2 + c) * chunks + k

    def turned(shift):
        return (bot + shift) % 2

    other_core = at(y, x, 1 - core)
    other_y = at(2 * top + 1 - bot, x, core)
    rel_peers = (other_core, other_y, at(3 - y, x, core), at(y, x + 1 - 2 * (x % 2), core), at(y, x_size - 1 - x, core), other_core)
    grad_to = place((mine + step) % groups, turned(step), core)
    grad_from = place((mine + groups - step) % groups, turned(step), core)
    nxt = step + 1
    table_to = place((mine + groups - nxt) % groups, turned(nxt), core)
    table_from = place((mine + nxt) % groups, turned(nxt), core)
    peers = list(rel_peers)
    if step:
        peers += [grad_to, grad_from]
    if last:
        for turn in range(4):
            peers.append(at((y + turn) % 4, x, top))
        senders = [at((2 * core + d), x, c) for d in range(2) for c in range(2)]
        peers += senders
    else:
        peers += [table_to, table_from]
    entry(peers)
    keep = turned(step)
    pending = []

    def start(copy):
        copy.start()
        pending.append(copy)
        return copy

    shards = [(1 - keep, k) for k in range(chunks)] + [(keep, k) for k in range(chunks)]
    loads, cores = [], []
    row_loads = [pltpu.make_async_copy(src, dst, row_sem.at[n]) for n, (src, dst) in enumerate(((head_hbm, head_ref), (ent_hbm, ent_ref)))]
    for load in row_loads:
        load.start()
    stores = []

    def store(n, src, dst):
        copy = pltpu.make_async_copy(src, dst, store_sem.at[n])
        copy.start()
        stores.append(copy)

    def store_table(low, c, k):
        slot = slot_of(low, c, k)
        store(slot, table.at[slot], table_hbm.at[slot])

    rel_copies = [start(remote(rel_grad_ref.at[1 - core], rel_from.at[0], rel_send.at[0], rel_recv.at[0], rel_peers[0]))]
    for n, (low, k) in enumerate(shards):
        cores.append(start(remote(tail_ref.at[slot_of(low, 1 - core, k)], from_core.at[n], core_send.at[n], core_recv.at[n], other_core)))
        load = pltpu.make_async_copy(tail_ref.at[slot_of(low, core, k)], own.at[n], own_sem.at[n])
        load.start()
        loads.append(load)

    def rel_step(n):
        rel_copies[n].wait_recv()
        rel_sum[n] = (rel_grad_ref[core] if n == 0 else rel_sum[n - 1]) + rel_from[n]
        rel_copies.append(start(remote(rel_sum.at[n], rel_from.at[n + 1], rel_send.at[n + 1], rel_recv.at[n + 1], rel_peers[n + 1])))

    ys = []
    for k in range(chunks):
        loads[k].wait()
        cores[k].wait_recv()
        own[k] = own[k] + from_core[k]
        ys.append(start(remote(own.at[k], from_y.at[k], y_send.at[k], y_recv.at[k], other_y)))
        if k == 1:
            rel_step(0)
    for k in range(chunks, 2 * chunks):
        loads[k].wait()
        cores[k].wait_recv()
        own[k] = own[k] + from_core[k]
    gs, outs, forwards, crosses = [], [], [], []

    def stage_group(k):
        ys[k].wait_recv()
        own[chunks + k] = own[chunks + k] + from_y[k]
        if step:
            gs.append(start(remote(own.at[chunks + k], from_group.at[k], group_send.at[k], group_recv.at[k], grad_to)))

    def cross_copy(k):
        return remote(send_buf.at[k], ent_wire.at[slot_of(bot, core, k)], out_send.at[2 * chunks + k], out_recv.at[slot_of(bot, core, k)], other_core)

    turn = (y + 4 - 2 * core) % 4
    near = 1 - turn % 2
    back = jnp.where((turn == 1) | (turn == 2), 0, 1)
    onward = at((y + 1 + 2 * back) % 4, x, core)

    def landed(low, c, k):
        slot = slot_of(low, c, k)
        remote(ent_wire.at[slot], ent_wire.at[slot], out_send.at[0], out_recv.at[slot], other_core).wait_recv()

    def stage_relay(k):
        if k % 2 == 0:
            return
        for c in CORES:
            landed(near, c, k - 1)
            landed(near, c, k)
            slot = slot_of(near, c, k) - 1 + back
            start(remote(ent_wire.at[slot], ent_wire.at[slot], out_send.at[(3 + c) * chunks + k], out_recv.at[slot], onward))

    def stage_update(k):
        if k == 0:
            for load in row_loads:
                load.wait()
        if step:
            gs[k].wait_recv()
        total = from_group if step else own
        base = k if step else chunks + k
        grad = [total[base, band(t, chunk), :] + head_ref[k, band(t, chunk), :] for t in TILES[:-1]]
        grad.append(below(unfold_last(total[base, 3 * chunk:, :] + head_ref[k, 3 * chunk:, :])))
        span = band(k, chunk)
        rows, state = adagrad(tiles_at(ent_ref, k * chunk, chunk), state_ref[span, :], grad, emb_width, learn_rate)
        wire = rows[:3] + [fold_last(rows[3])]
        if last:
            lane = lanes((chunk, LANES))
            wire.append(fold_last(jnp.where(lane < 1, state, 0.0)))
        else:
            wide = band(k, 4 * chunk)
            ent_ref[wide, :] = stack_tiles(rows)
            store(4 * chunks + k, ent_ref.at[wide], ent_out.at[wide])
            state_out[span, :] = state
        offset = 0
        for piece in wire:
            send_buf[k, offset:offset + piece.shape[0], :] = piece.astype(send_buf.dtype)
            offset += piece.shape[0]
        slot = slot_of(bot, core, k)
        if last:
            for n, turn in enumerate((1, 3)):
                start(remote(send_buf.at[k], ent_wire.at[slot], out_send.at[n * chunks + k], out_recv.at[slot], at((y + turn) % 4, x, top)))

            @pl.when(core == top)
            def _():
                pltpu.make_async_copy(send_buf.at[k], ent_wire.at[slot], out_recv.at[slot]).start()

            @pl.when(core != top)
            def _():
                cross_copy(k).start()
        else:
            outs.append(start(remote(send_buf.at[k], table.at[slot], out_send.at[k], out_recv.at[k], table_to)))

    def forward(n, low, k, peer):
        slot = slot_of(low, core, k)
        return start(remote(table.at[slot], table.at[slot], out_send.at[n * chunks + k], out_recv.at[n * chunks + k], peer))

    def stage_forward(k):
        outs[k].wait_recv()
        store_table(turned(nxt), core, k)
        forwards.append(forward(1, turned(nxt), k, other_y))
        crosses.append(forward(2, turned(nxt), k, other_core))

    def stage_cross(k):
        forwards[k].wait_recv()
        store_table(1 - turned(nxt), core, k)
        crosses.append(forward(3, 1 - turned(nxt), k, other_core))

    stages = (stage_group, stage_update, stage_relay) if last else (stage_group, stage_update, stage_forward, stage_cross)
    rel_steps = len(rel_peers) - 1
    for tick in range(chunks + LAG * (len(stages) - 1)):
        for n, stage in enumerate(stages):
            if 0 <= tick - LAG * n < chunks:
                stage(tick - LAG * n)
        if tick % 2 == 1 and tick < 2 * rel_steps - 1:
            rel_step(tick // 2 + 1)

    rel_copies[rel_steps].wait_recv()
    halves = rel_sum[rel_steps - 1], rel_from[rel_steps]
    summed = below([jnp.where(core == n, halves[0], halves[1]) for n in CORES])
    rel_grad = [summed[band(t, REL_PAD)] for t in TILES[:-1]] + [below(unfold_last(summed[3 * REL_PAD:]))]
    loss_out[...] = rel_grad[0][REL_PAD - 1:, :]
    row = sublanes((REL_PAD, LANES))
    rel_grad[0] = jnp.where(row < REL_PAD - 1, rel_grad[0], 0.0)
    rel_rows, rel_state = adagrad(tiles_of(rel_ref[...]), rel_state_ref[...], rel_grad, emb_width, learn_rate)
    for t in TILES:
        rel_out[:, band(t, LANES)] = rel_rows[t]
    if not last:
        rel_state_out[...] = rel_state

    if last:
        for c in CORES:
            for k in range(chunks):
                landed(1 - near, c, k)

        @pl.when(core != top)
        def _():
            for k in range(chunks):
                cross_copy(k).wait_send()
    else:
        for n, copy in enumerate(crosses):
            copy.wait_recv()
        for low in CORES:
            for k in range(chunks):
                store_table(low, 1 - core, k)
        for copy in stores:
            copy.wait()
    for copy in pending:
        copy.wait_send()


def exchange_call(step, groups, emb_width, tail, head, rel_grad, ent, state, rel, rel_state):
    vmem, hbm = pl.BlockSpec(memory_space=pltpu.VMEM), pl.BlockSpec(memory_space=pl.ANY)
    chunks = head.shape[0]
    rel_grad = rel_grad.reshape(2, -1, LANES)
    wire = wire_rows(CHUNK)
    last = step == groups - 1
    like = lambda x: jax.ShapeDtypeStruct(x.shape, x.dtype)
    loss = jax.ShapeDtypeStruct((1, LANES), F32)
    out_wire = wire + (CHUNK // LEFT if last else 0)
    out_type = F32 if last else BF16
    gathered = jax.ShapeDtypeStruct((4 * chunks, out_wire, LANES), out_type)
    out_shape = (gathered, like(rel), loss) if last else (like(ent), like(state), like(rel), like(rel_state), loss, gathered)
    return pl.pallas_call(
        functools.partial(exchange_kernel, (step, groups, chunks, emb_width, last)),
        out_shape=out_shape,
        in_specs=[hbm, hbm, vmem, hbm, vmem, vmem, vmem],
        out_specs=(vmem,) * 3 if last else (hbm, vmem, vmem, vmem, vmem, hbm),
        scratch_shapes=[
            pltpu.VMEM((2 * chunks, wire, LANES), F32), pltpu.VMEM((2 * chunks, wire, LANES), F32),
            pltpu.VMEM((chunks, wire, LANES), F32), pltpu.VMEM((chunks, wire, LANES), F32),
            pltpu.VMEM((REL_HOPS - 1, *rel_grad.shape[1:]), F32), pltpu.VMEM((REL_HOPS, *rel_grad.shape[1:]), F32),
            pltpu.VMEM((chunks, out_wire, LANES), out_type),
            *[dma_sems(2 * chunks)] * 3, *[dma_sems(chunks)] * 4,
            dma_sems(REL_HOPS), dma_sems(REL_HOPS), dma_sems(5 * chunks), dma_sems(4 * chunks),
            pltpu.VMEM(head.shape, F32), pltpu.VMEM(ent.shape, F32), dma_sems(2),
            *(() if last else (pltpu.VMEM(gathered.shape, BF16), dma_sems(5 * chunks))),
        ],
        compiler_params=pltpu.CompilerParams(vmem_limit_bytes=VMEM_LIMIT, collective_id=step, has_side_effects=True),
        name='exchange',
    )(tail, head, rel_grad, ent, state, rel, rel_state)


def setup_kernel(cfg, head_ref, tail_ref, rel_id_ref, mask_ref, neg_ref, ent_hbm, rel_ref, word_out, rel_id_out, count_out, neg_out, table, ent_out, rel_out,
                 packed, shares, neg_buf, rows_buf, away, send_sem, recv_sem, core_send, core_recv, load_sem, table_send, table_recv):
    head_bits, tail_bits, spare = cfg
    y, x, core, top, bot = where_here()
    home = core == top
    other_core = {'data': y, 'ent': 2 * x + 1 - core}
    users = [(c, 2 * core + d) for c in CORES for d in CORES]
    users = [({'data': row, 'ent': 2 * x + c}, (core == c) & (y == row)) for c, row in users]
    entry([peer for peer, _ in users] + [{'data': row, 'ent': 2 * x + top} for row in TILES] + [other_core])
    edges = head_ref[...] | (tail_ref[...] << tail_bits) | (rel_id_ref[...] << (2 * tail_bits))
    packed[...] = jnp.where(mask_ref[...] > 0, edges, spare << (2 * tail_bits))
    neg_buf[:, 0, :] = row_address(neg_ref[...])
    to_users = [remote(packed, shares.at[y], send_sem.at[n], recv_sem.at[y], peer) for n, (peer, _) in enumerate(users)]
    for copy, (_, here) in zip(to_users, users):
        @pl.when(jnp.logical_not(here))
        def _():
            copy.start()

    chunks, chunk = table.shape[0], CHUNK
    shard = chunks // 4

    def load(n):
        return pltpu.make_async_copy(ent_hbm.at[:, pl.ds(pl.multiple_of(n * chunk, chunk), chunk)], rows_buf.at[n % 4], load_sem.at[n % 4])

    def table_copy(q):
        part = table.at[pl.ds(q * shard, shard)]
        return remote(part, part, table_send.at[q], table_recv.at[q], other_core)

    neg_copy = remote(neg_buf, neg_out, core_send.at[0], core_recv.at[0], other_core)
    ent_copy = remote(away, ent_out, core_send.at[1], core_recv.at[1], other_core)

    @pl.when(home)
    def _():
        pltpu.make_async_copy(packed, shares.at[y], recv_sem.at[y]).start()
        neg_copy.start()
        neg_out[...] = neg_buf[...]
        for n in range(3):
            load(n).start()
        for q in TILES:
            def one(k, carry):
                n = q * shard + k

                @pl.when(n + 3 < chunks)
                def _():
                    load(n + 3).start()

                load(n).wait()
                tiles = columns_to_tiles(rows_buf[n % 4])
                for t in TILES[:-1]:
                    table[n, band(t, chunk), :] = tiles[t].astype(BF16)
                table[n, 3 * chunk:, :] = fold_last(tiles[3]).astype(BF16)
                place = pl.ds(pl.multiple_of(k * chunk * 4, chunk * 4), chunk * 4)

                @pl.when(2 * bot + core == q)
                def _():
                    ent_out[place, :] = stack_tiles(tiles)

                @pl.when(2 * bot + 1 - core == q)
                def _():
                    away[place, :] = stack_tiles(tiles)

                return carry

            lax.fori_loop(0, shard, one, 0)
            table_copy(q).start()

            @pl.when(2 * bot + 1 - core == q)
            def _():
                ent_copy.start()

    for t, tile in enumerate(columns_to_tiles(rel_ref[...])):
        rel_out[:, band(t, LANES)] = tile
    for row in TILES:
        remote(packed, shares.at[row], send_sem.at[0], recv_sem.at[row], other_core).wait_recv()
    share = beside([shares[row] for row in TILES])
    mine = ((share >> head_bits) & 3 == 2 * bot + core) & (share >> (2 * tail_bits) != spare)
    lane = lanes(share.shape)
    width = share.shape[1]
    steps = (width - 1).bit_length()
    other = jnp.where(mine, 0, 1)
    before = other
    for bit in range(steps):
        before = before + jnp.where(lane < 2**bit, 0, roll(before, 2**bit))
    count_out[...] = jnp.broadcast_to(width - before[:, width - 1:], count_out.shape)
    none = spare << (head_bits + tail_bits)
    edge = jnp.where(mine, (share & (2**head_bits - 1)) | (share >> tail_bits << head_bits), none)
    shift = jnp.where(mine, before - other, 0)
    for bit in range(steps):
        here = (shift >> bit) & 1 == 1
        edge_in, shift_in = roll(edge, width - 2**bit), roll(shift, width - 2**bit)
        there = (shift_in >> bit) & 1 == 1
        edge = jnp.where(there, edge_in, jnp.where(here, none, edge))
        shift = jnp.where(there, shift_in, jnp.where(here, 0, shift))
    rel_id_out[:, 0, :] = edge >> (head_bits + tail_bits)
    head, tail = edge & (2**head_bits - 1), (edge >> head_bits) & (2**tail_bits - 1)
    margin = jnp.zeros((share.shape[0], BLOCK), jnp.int32)
    word_out[:, 0, :] = beside([margin, (row_address(head) << (tail_bits + 2)) | row_address(tail), margin])
    for copy, (_, here) in zip(to_users, users):
        @pl.when(jnp.logical_not(here))
        def _():
            copy.wait_send()

    between = [neg_copy, ent_copy, *(table_copy(q) for q in TILES)]

    @pl.when(home)
    def _():
        for copy in between:
            copy.wait_send()

    @pl.when(jnp.logical_not(home))
    def _():
        for copy in between:
            copy.wait_recv()


def setup_call(cfg, head, tail, rel_ids, mask, neg, reps, ent, rel):
    vmem, hbm = pl.BlockSpec(memory_space=pltpu.VMEM), pl.BlockSpec(memory_space=pl.ANY)
    groups, share = head.shape
    width, rows = ent.shape
    chunks = rows // CHUNK
    return pl.pallas_call(
        functools.partial(setup_kernel, cfg),
        out_shape=(*(jax.ShapeDtypeStruct(shape, jnp.int32) for shape in ((groups, 1, reps * share + 2 * BLOCK), (groups, 1, reps * share), (groups, LANES), (groups, 1, neg.shape[1]))),
                   jax.ShapeDtypeStruct((chunks, wire_rows(CHUNK), LANES), BF16), jax.ShapeDtypeStruct((rows, LANES), F32), jax.ShapeDtypeStruct((REL_PAD, 4 * LANES), F32)),
        in_specs=[*[vmem] * 5, hbm, vmem],
        out_specs=(vmem,) * 7,
        scratch_shapes=[pltpu.VMEM(head.shape, jnp.int32), pltpu.VMEM((reps, *head.shape), jnp.int32), pltpu.VMEM((groups, 1, neg.shape[1]), jnp.int32),
                        pltpu.VMEM((4, width, CHUNK), F32), pltpu.VMEM((rows, LANES), F32), *[dma_sems(4)] * 2, *[dma_sems(2)] * 2, *[dma_sems(4)] * 3],
        compiler_params=pltpu.CompilerParams(collective_id=20, has_side_effects=True),
        name='setup',
    )(head, tail, rel_ids, mask, neg, ent, rel)


def finish_kernel(wire_ref, rel_ref, ent_out, state_out, rel_out):
    chunk = CHUNK
    for n in range(wire_ref.shape[0]):
        tiles = [wire_ref[n, band(t, chunk), :] for t in TILES[:-1]]
        tiles.append(below(unfold_last(wire_ref[n, 3 * chunk:wire_rows(chunk), :])))
        ent_out[:, band(n, chunk)] = tiles_to_columns(tiles)
        state = below([part[:, :1] for part in unfold_last(wire_ref[n, wire_rows(chunk):, :])])
        state_out[:, band(n, chunk)] = jnp.broadcast_to(state, (chunk, LANES)).T[:1]

    @pl.when(pl.program_id(0) == 0)
    def _():
        rel_out[...] = tiles_to_columns(tiles_of(rel_ref[...]))


def finish_call(wire, rel, width):
    chunks = wire.shape[0]
    size = chunks // 8
    whole = lambda n: (0, 0)
    return pl.pallas_call(
        finish_kernel,
        out_shape=tuple(jax.ShapeDtypeStruct(shape, F32) for shape in ((width, chunks * CHUNK), (1, chunks * CHUNK), (width, REL_PAD))),
        grid=(chunks // size,),
        in_specs=[pl.BlockSpec((size, *wire.shape[1:]), lambda n: (n, 0, 0)), pl.BlockSpec(rel.shape, whole)],
        out_specs=(pl.BlockSpec((width, size * CHUNK), lambda n: (0, n)), pl.BlockSpec((1, size * CHUNK), lambda n: (0, n)), pl.BlockSpec((width, REL_PAD), whole)),
        name='finish',
    )(wire, rel)


def solution(mesh):
    groups = mesh.shape['ent']
    data_reps = mesh.shape['data']
    row_spec = P(('sweep', 'ent'), None)
    edge_spec = P(('sweep', 'ent'), None, 'data')

    def device_fn(ent_table, ent_state, rel_table, head_idx, tail_idx, rel_idx, edge_mask, neg_idx):
        part_rows, emb_width = ent_table.shape
        rel_rows = rel_table.shape[0]
        bucket_edges = head_idx.shape[2] * data_reps
        shard = part_rows // 4
        tail_bits = (part_rows - 1).bit_length()
        head_bits = (shard - 1).bit_length()
        spare = 2**(REL_PAD - 1).bit_length() - 1
        ent = lax.axis_index('ent')
        _, _, core, top, bot = where_here()

        words, rel_ids, counts, neg, table, ent_now, rel_now = setup_call(
            (head_bits, tail_bits, spare), head_idx[0], tail_idx[0], rel_idx[0], edge_mask[0], neg_idx[0], data_reps,
            ent_table.T, jnp.pad(rel_table.T, ((0, 0), (0, REL_PAD - rel_rows))))
        to_core = lambda c: lax.dynamic_slice_in_dim(ent_state, (2 * bot + c) * shard, shard)
        away = [(d * groups + 2 * (n // 2) + d // 2, d * groups + 2 * (n // 2) + 1 - d // 2) for d in range(data_reps) for n in range(0, groups, 2)]
        state_now = jnp.where(core == top, to_core(core), lax.ppermute(to_core(1 - core), ('data', 'ent'), away))[:, None]
        rel_state = jnp.zeros((REL_PAD, 1), F32)
        losses = []
        for step in range(groups):
            tail, head, rel_grad = bucket_call(step, tail_bits + 2, words, counts, neg, rel_ids, ent_now, rel_now, table)
            out = exchange_call(step, groups, emb_width, tail, head, rel_grad, ent_now, state_now, rel_now, rel_state)
            if step + 1 < groups:
                ent_now, state_now, rel_now, rel_state, loss, table = out
            else:
                wire, rel_now, loss = out
            losses.append(loss)
        ent_out, state_out, rel_out = finish_call(wire, rel_now, emb_width)
        loss_rows = below(losses) / bucket_edges
        bucket_loss = lax.dynamic_slice_in_dim(loss_rows, ent, 1, axis=1).reshape(1, groups)
        return ent_out.T, state_out[0], rel_out[:, :rel_rows].T, bucket_loss

    return jax.shard_map(device_fn, mesh=mesh, in_specs=(row_spec, P(('sweep', 'ent')), P('sweep', None), edge_spec, edge_spec, edge_spec, edge_spec, P(('sweep', 'ent'), None, None)), out_specs=(row_spec, P(('sweep', 'ent')), P('sweep', None), row_spec), check_vma=False)
```

profile of v0, /device:TPU:97, one launch (start us, length us, event | category | flops | bytes accessed | tf_op | source)
XLA Modules:
  0.0 998.3 jit_solution(17062913407727845195)
XLA Ops:
  0.7 0.7 dynamic_slice.10
  1.4 1.3 collective-permute-start
  2.7 1.6 pad.4.rel_ref
  4.3 22.8 %setup.1 = (s32[8,1,8704]{2,1,0:T(1,128)}, s32[8,1,8192]{2,1,0:T(1,128)}, s32[8,128]{1,0:T(8,128)}, s32[8,1,1024]{2,1,0:T(1,128)}, bf16[32,400,128]{2,1,0:T(8,12...) custom-call(s32[8,2048]{1,0:T(8,128)} %bitcast.31, s32[8,2048]{1,0:T(8,128)} %bitcast.32, s32[8,2048]{1,0:T(8,128)} %bitcast.33, ...), custom_call_target="tpu_custom_call" | custom-call | tf_op jit(solution)/shard_map/setup/pallas_call | solution.py:786
  27.1 33.9 %bucket.8 = (f32[32,400,128]{2,1,0:T(8,128)}, f32[8,400,128]{2,1,0:T(8,128)}, f32[400,128]{1,0:T(8,128)}) custom-call(s32[8,1,8704]{2,1,0:T(1,128)} %get-tuple-element.83.edges_hbm, s32[8,128]{1,0:T(8,128)} %get-tuple-element.84.count_ref, s32[8,1,1024]{2,1,0:T(1,128)} %get-tuple-element.85.negs_hbm, s32[8,1,8192]{2,1,0:T(1,128)} %get-tuple-element.86.rel_ids_hbm, ...), custom_call_target="tpu_custom_call" | custom-call | tf_op jit(solution)/shard_map/bucket/pallas_call | solution.py:372
  61.0 0.0 collective-permute-done
  61.0 0.7 dynamic-slice_select_fusion
  61.7 1.0 copy.12.state_ref
  62.8 0.6 broadcast_in_dim.7.rel_state_ref
  63.4 78.3 %exchange.8 = (f32[4096,128]{1,0:T(8,128)}, f32[1024,1]{1,0:T(8,128)}, f32[128,512]{1,0:T(8,128)}, f32[128,1]{1,0:T(8,128)}, f32[1,128]{1,0:T(1,128)}, /*index=5*/bf16[32,400,128]{2,1,0:T(8,128)(2,1)}) custom-call(f32[32,400,128]{2,1,0:T(8,128)} %get-tuple-element.90.tail_ref, f32[8,400,128]{2,1,0:T(8,128)} %get-tuple-element.91.head_hbm, ...), custom_call_target="tpu_custom_call" | custom-call | tf_op jit(solution)/shard_map/exchange/pallas_call | solution.py:646
  141.7 17.7 %bucket.9 = (f32[32,400,128]{2,1,0:T(8,128)}, f32[8,400,128]{2,1,0:T(8,128)}, f32[400,128]{1,0:T(8,128)}) custom-call(s32[8,1,8704]{2,1,0:T(1,128)} %get-tuple-element.83.edges_hbm, s32[8,128]{1,0:T(8,128)} %get-tuple-element.84.count_ref, s32[8,1,1024]{2,1,0:T(1,128)} %get-tuple-element.85.negs_hbm, s32[8,1,8192]{2,1,0:T(1,128)} %get-tuple-element.86.rel_ids_hbm, ...), custom_call_target="tpu_custom_call" | custom-call | tf_op jit(solution)/shard_map/bucket/pallas_call | solution.py:372
  159.4 83.1 %exchange.9 = (f32[4096,128]{1,0:T(8,128)}, f32[1024,1]{1,0:T(8,128)}, f32[128,512]{1,0:T(8,128)}, f32[128,1]{1,0:T(8,128)}, f32[1,128]{1,0:T(1,128)}, /*index=5*/bf16[32,400,128]{2,1,0:T(8,128)(2,1)}) custom-call(f32[32,400,128]{2,1,0:T(8,128)} %get-tuple-element.96.tail_ref, f32[8,400,128]{2,1,0:T(8,128)} %get-tuple-element.97.head_hbm, ...), custom_call_target="tpu_custom_call" | custom-call | tf_op jit(solution)/shard_map/exchange/pallas_call | solution.py:646
  242.5 34.3 %bucket.10 = (f32[32,400,128]{2,1,0:T(8,128)}, f32[8,400,128]{2,1,0:T(8,128)}, f32[400,128]{1,0:T(8,128)}) custom-call(s32[8,1,8704]{2,1,0:T(1,128)} %get-tuple-element.83.edges_hbm, s32[8,128]{1,0:T(8,128)} %get-tuple-element.84.count_ref, s32[8,1,1024]{2,1,0:T(1,128)} %get-tuple-element.85.negs_hbm, s32[8,1,8192]{2,1,0:T(1,128)} %get-tuple-element.86.rel_ids_hbm, ...), custom_call_target="tpu_custom_call" | custom-call | tf_op jit(solution)/shard_map/bucket/pallas_call | solution.py:372
  276.8 97.5 %exchange.10 = (f32[4096,128]{1,0:T(8,128)}, f32[1024,1]{1,0:T(8,128)}, f32[128,512]{1,0:T(8,128)}, f32[128,1]{1,0:T(8,128)}, f32[1,128]{1,0:T(1,128)}, /*index=5*/bf16[32,400,128]{2,1,0:T(8,128)(2,1)}) custom-call(f32[32,400,128]{2,1,0:T(8,128)} %get-tuple-element.104.tail_ref, f32[8,400,128]{2,1,0:T(8,128)} %get-tuple-element.105.head_hbm, ...), custom_call_target="tpu_custom_call" | custom-call | tf_op jit(solution)/shard_map/exchange/pallas_call | solution.py:646
  374.3 20.9 %bucket.11 = (f32[32,400,128]{2,1,0:T(8,128)}, f32[8,400,128]{2,1,0:T(8,128)}, f32[400,128]{1,0:T(8,128)}) custom-call(s32[8,1,8704]{2,1,0:T(1,128)} %get-tuple-element.83.edges_hbm, s32[8,128]{1,0:T(8,128)} %get-tuple-element.84.count_ref, s32[8,1,1024]{2,1,0:T(1,128)} %get-tuple-element.85.negs_hbm, s32[8,1,8192]{2,1,0:T(1,128)} %get-tuple-element.86.rel_ids_hbm, ...), custom_call_target="tpu_custom_call" | custom-call | tf_op jit(solution)/shard_map/bucket/pallas_call | solution.py:372
  395.2 90.0 %exchange.11 = (f32[4096,128]{1,0:T(8,128)}, f32[1024,1]{1,0:T(8,128)}, f32[128,512]{1,0:T(8,128)}, f32[128,1]{1,0:T(8,128)}, f32[1,128]{1,0:T(1,128)}, /*index=5*/bf16[32,400,128]{2,1,0:T(8,128)(2,1)}) custom-call(f32[32,400,128]{2,1,0:T(8,128)} %get-tuple-element.112.tail_ref, f32[8,400,128]{2,1,0:T(8,128)} %get-tuple-element.113.head_hbm, ...), custom_call_target="tpu_custom_call" | custom-call | tf_op jit(solution)/shard_map/exchange/pallas_call | solution.py:646
  485.2 17.6 %bucket.12 = (f32[32,400,128]{2,1,0:T(8,128)}, f32[8,400,128]{2,1,0:T(8,128)}, f32[400,128]{1,0:T(8,128)}) custom-call(s32[8,1,8704]{2,1,0:T(1,128)} %get-tuple-element.83.edges_hbm, s32[8,128]{1,0:T(8,128)} %get-tuple-element.84.count_ref, s32[8,1,1024]{2,1,0:T(1,128)} %get-tuple-element.85.negs_hbm, s32[8,1,8192]{2,1,0:T(1,128)} %get-tuple-element.86.rel_ids_hbm, ...), custom_call_target="tpu_custom_call" | custom-call | tf_op jit(solution)/shard_map/bucket/pallas_call | solution.py:372
  502.8 111.8 %exchange.12 = (f32[4096,128]{1,0:T(8,128)}, f32[1024,1]{1,0:T(8,128)}, f32[128,512]{1,0:T(8,128)}, f32[128,1]{1,0:T(8,128)}, f32[1,128]{1,0:T(1,128)}, /*index=5*/bf16[32,400,128]{2,1,0:T(8,128)(2,1)}) custom-call(f32[32,400,128]{2,1,0:T(8,128)} %get-tuple-element.120.tail_ref, f32[8,400,128]{2,1,0:T(8,128)} %get-tuple-element.121.head_hbm, ...), custom_call_target="tpu_custom_call" | custom-call | tf_op jit(solution)/shard_map/exchange/pallas_call | solution.py:646
  614.7 28.7 %bucket.13 = (f32[32,400,128]{2,1,0:T(8,128)}, f32[8,400,128]{2,1,0:T(8,128)}, f32[400,128]{1,0:T(8,128)}) custom-call(s32[8,1,8704]{2,1,0:T(1,128)} %get-tuple-element.83.edges_hbm, s32[8,128]{1,0:T(8,128)} %get-tuple-element.84.count_ref, s32[8,1,1024]{2,1,0:T(1,128)} %get-tuple-element.85.negs_hbm, s32[8,1,8192]{2,1,0:T(1,128)} %get-tuple-element.86.rel_ids_hbm, ...), custom_call_target="tpu_custom_call" | custom-call | tf_op jit(solution)/shard_map/bucket/pallas_call | solution.py:372
  643.4 89.7 %exchange.13 = (f32[4096,128]{1,0:T(8,128)}, f32[1024,1]{1,0:T(8,128)}, f32[128,512]{1,0:T(8,128)}, f32[128,1]{1,0:T(8,128)}, f32[1,128]{1,0:T(1,128)}, /*index=5*/bf16[32,400,128]{2,1,0:T(8,128)(2,1)}) custom-call(f32[32,400,128]{2,1,0:T(8,128)} %get-tuple-element.128.tail_ref, f32[8,400,128]{2,1,0:T(8,128)} %get-tuple-element.129.head_hbm, ...), custom_call_target="tpu_custom_call" | custom-call | tf_op jit(solution)/shard_map/exchange/pallas_call | solution.py:646
  733.1 26.1 %bucket.14 = (f32[32,400,128]{2,1,0:T(8,128)}, f32[8,400,128]{2,1,0:T(8,128)}, f32[400,128]{1,0:T(8,128)}) custom-call(s32[8,1,8704]{2,1,0:T(1,128)} %get-tuple-element.83.edges_hbm, s32[8,128]{1,0:T(8,128)} %get-tuple-element.84.count_ref, s32[8,1,1024]{2,1,0:T(1,128)} %get-tuple-element.85.negs_hbm, s32[8,1,8192]{2,1,0:T(1,128)} %get-tuple-element.86.rel_ids_hbm, ...), custom_call_target="tpu_custom_call" | custom-call | tf_op jit(solution)/shard_map/bucket/pallas_call | solution.py:372
  759.2 73.4 %exchange.14 = (f32[4096,128]{1,0:T(8,128)}, f32[1024,1]{1,0:T(8,128)}, f32[128,512]{1,0:T(8,128)}, f32[128,1]{1,0:T(8,128)}, f32[1,128]{1,0:T(1,128)}, /*index=5*/bf16[32,400,128]{2,1,0:T(8,128)(2,1)}) custom-call(f32[32,400,128]{2,1,0:T(8,128)} %get-tuple-element.136.tail_ref, f32[8,400,128]{2,1,0:T(8,128)} %get-tuple-element.137.head_hbm, ...), custom_call_target="tpu_custom_call" | custom-call | tf_op jit(solution)/shard_map/exchange/pallas_call | solution.py:646
  832.6 31.2 %bucket.15 = (f32[32,400,128]{2,1,0:T(8,128)}, f32[8,400,128]{2,1,0:T(8,128)}, f32[400,128]{1,0:T(8,128)}) custom-call(s32[8,1,8704]{2,1,0:T(1,128)} %get-tuple-element.83.edges_hbm, s32[8,128]{1,0:T(8,128)} %get-tuple-element.84.count_ref, s32[8,1,1024]{2,1,0:T(1,128)} %get-tuple-element.85.negs_hbm, s32[8,1,8192]{2,1,0:T(1,128)} %get-tuple-element.86.rel_ids_hbm, ...), custom_call_target="tpu_custom_call" | custom-call | tf_op jit(solution)/shard_map/bucket/pallas_call | solution.py:372
  863.8 0.0 copy-start
  863.8 0.0 copy-start.1
  863.8 0.0 copy-start.2
  863.8 0.0 copy-start.3
  863.9 120.1 %exchange.15 = (f32[32,416,128]{2,1,0:T(8,128)}, f32[128,512]{1,0:T(8,128)}, f32[1,128]{1,0:T(1,128)}) custom-call(f32[32,400,128]{2,1,0:T(8,128)} %get-tuple-element.144.tail_ref, f32[8,400,128]{2,1,0:T(8,128)} %get-tuple-element.145.head_hbm, f32[2,200,128]{2,1,0:T(8,128)} %bitcast.23, f32[4096,128]{1,0:T(8,128)} %get-tuple-element.141.ent_hbm, ...), custom_call_target="tpu_custom_call" | custom-call | tf_op jit(solution)/shard_map/exchange/pallas_call | solution.py:646
  984.1 0.6 concatenate.3
  984.7 10.9 %finish.1 = (f32[400,4096]{1,0:T(8,128)}, f32[1,4096]{1,0:T(1,128)}, f32[400,128]{1,0:T(8,128)}) custom-call(f32[32,416,128]{2,1,0:T(8,128)} %get-tuple-element.149.wire_ref, f32[128,512]{1,0:T(8,128)} %get-tuple-element.150.rel_ref), custom_call_target="tpu_custom_call" | custom-call | tf_op jit(solution)/shard_map/finish/pallas_call | solution.py:817
  995.6 1.6 slice_bitcast_fusion
  997.2 0.7 dynamic-slice_reduce_fusion
  (11 shorter events, 0.0 us)
Async XLA Ops:
  1.4 59.7 %collective-permute-start = (f32[1024]{0:T(1024)S(1)}, f32[1024]{0:T(1024)S(1)}, u32[]{:S(2)}, u32[]{:S(2)}) collective-permute-start(f32[1024]{0:T(1024)S(1)} %dynamic_slice.10), channel_id=1, source_target_pairs={{0,1},{2,3},{4,5},{6,7},{8,9},{10,11},{12,13},{14,15},{17,16},{19,... | collective-permute-start | bytes 12296 | tf_op jit(solution)/shard_map/ppermute | solution.py:849
  863.8 120.2 %copy-start = (f32[1,128]{1,0:T(1,128)S(1)}, f32[1,128]{1,0:T(1,128)}, u32[]{:S(2)}) copy-start(f32[1,128]{1,0:T(1,128)} %get-tuple-element.154) | copy-start | bytes 1540
  863.8 120.2 %copy-start.1 = (f32[1,128]{1,0:T(1,128)S(1)}, f32[1,128]{1,0:T(1,128)}, u32[]{:S(2)}) copy-start(f32[1,128]{1,0:T(1,128)} %get-tuple-element.155) | copy-start | bytes 1540
  863.8 120.2 %copy-start.2 = (f32[1,128]{1,0:T(1,128)S(1)}, f32[1,128]{1,0:T(1,128)}, u32[]{:S(2)}) copy-start(f32[1,128]{1,0:T(1,128)} %get-tuple-element.156) | copy-start | bytes 1540
  863.8 120.2 %copy-start.3 = (f32[1,128]{1,0:T(1,128)S(1)}, f32[1,128]{1,0:T(1,128)}, u32[]{:S(2)}) copy-start(f32[1,128]{1,0:T(1,128)} %get-tuple-element.157) | copy-start | bytes 1540
  863.9 120.2 %copy-start.4 = (f32[1,128]{1,0:T(1,128)S(1)}, f32[1,128]{1,0:T(1,128)}, u32[]{:S(2)}) copy-start(f32[1,128]{1,0:T(1,128)} %get-tuple-element.158) | copy-start | bytes 1540
  863.9 120.2 %copy-start.5 = (f32[1,128]{1,0:T(1,128)S(1)}, f32[1,128]{1,0:T(1,128)}, u32[]{:S(2)}) copy-start(f32[1,128]{1,0:T(1,128)} %get-tuple-element.159) | copy-start | bytes 1540
  863.9 120.2 %copy-start.6 = (f32[1,128]{1,0:T(1,128)S(1)}, f32[1,128]{1,0:T(1,128)}, u32[]{:S(2)}) copy-start(f32[1,128]{1,0:T(1,128)} %get-tuple-element.160) | copy-start | bytes 1540
where the time goes:
time: 1010 us; the launch traced here: 998 us
  Pallas kernels  988 us (98%)
    pallas_call x8, Pallas kernels, exchange_call(): pl.pallas_call(functools.partial(exchange_kernel, (step, groups, chunks,...  744 us
    pallas_call x8, Pallas kernels, bucket_call(): pl.pallas_call(functools.partial(bucket_kernel, (step, tail_bits)), out_s...  210 us
    pallas_call x1, Pallas kernels, setup_call(): pl.pallas_call(functools.partial(setup_kernel, cfg), out_shape=(*(jax.Sha...  22.8 us
  transfers between devices with their start and end apart: 1, of which 0 were waited for; matrix products, arithmetic and copies ran while one was open for 0% of the time, Pallas kernels for 6%

commit v1 on v0

--- a/solution.py
+++ b/solution.py
@@ -16,7 +16,8 @@
 CHUNK = 128
 UNROLL = 64
 ROLLED = 32
-TOGETHER = 4
+TOGETHER = 8
+AHEAD = 6
 LAG = 3
 PARTS = 4
 REL_HOPS = 6
@@ -50,12 +51,32 @@
     return lax.broadcasted_iota(jnp.int32, shape, 0)
 
 
+def one_where(mask):
+    return jnp.where(mask, 1.0, 0.0)
+
+
+def on_diagonal(size):
+    return sublanes((size, size)) == lanes((size, size))
+
+
 def row_sum(x):
     return jnp.sum(x, axis=1, keepdims=True)
 
 
+def column_sum(x):
+    return jnp.sum(x, axis=0, keepdims=True)
+
+
 def wire_rows(rows):
     return 3 * rows + rows // LEFT
+
+
+def flipped(tiles):
+    rows, columns = tiles[0].shape
+    unit = one_where(on_diagonal(columns)).astype(BF16)
+    high, mid, low = (dot(unit, piece, ROW_ROW) for piece in in_three(below(tiles)))
+    both = high + mid + low
+    return [both[:, band(t, rows)] for t in TILES]
 
 
 def columns_to_tiles(x):
@@ -63,11 +84,11 @@
     a, c, d = slice(0, LANES), slice(LANES, LANES + HALF), slice(LANES + HALF, half)
     re, im = x[:half], x[half:]
     zero = jnp.zeros((HALF - LEFT, x.shape[1]), x.dtype)
-    return [t.T for t in (re[a], im[a], below([re[c], im[c]]), below([re[d], zero, im[d], zero]))]
+    return flipped([re[a], im[a], below([re[c], im[c]]), below([re[d], zero, im[d], zero])])
 
 
 def tiles_to_columns(tiles):
-    a, b, c, d = (t.T for t in tiles)
+    a, b, c, d = flipped(tiles)
     high = slice(HALF, HALF + LEFT)
     return below([a, c[:HALF], d[:LEFT], b, c[HALF:], d[high]])
 
@@ -264,7 +285,7 @@
     def block(n, carry):
         base = pl.multiple_of(n * BLOCK, BLOCK)
         hot = sublanes((REL_PAD, BLOCK)) == rel_id_ref[:, pl.ds(base, BLOCK)]
-        hot = jnp.where(hot, 1.0, 0.0).astype(BF16)
+        hot = one_where(hot).astype(BF16)
         rel_buf[...] = dot(below([hot] * 3), rel_three[...], COL_COL)
         for span in spans:
             head, tail, rel = tiles_at(head_next, span.start, STRIP), tiles_at(tail_next, span.start, STRIP), tiles_of(rel_buf[span, :])
@@ -281,13 +302,13 @@
         each_row(BLOCK // 2, put_edges(base))
         score_buf[...] = dot(query_buf[...], neg_rows[...], ROW_ROW)
         for span in spans:
-            weight = jnp.where(sublanes((STRIP, 1)) + (base + span.start) < count, 1.0, 0.0)
+            weight = one_where(sublanes((STRIP, 1)) + (base + span.start) < count)
             score, pos = score_buf[span, :], pos_buf[span, :]
             top = jnp.maximum(jnp.max(score, axis=1, keepdims=True), pos)
             pos_exp = jnp.exp(pos - top)
             neg_exp = jnp.exp(score - top)
             total = pos_exp + row_sum(neg_exp)
-            loss_acc[...] += jnp.sum(weight * (top + jnp.log(total) - pos), axis=0, keepdims=True)
+            loss_acc[...] += column_sum(weight * (top + jnp.log(total) - pos))
             pos_buf[span, :] = weight * (pos_exp / total - 1.0)
             d_neg_buf[span, :] = ((weight / total) * neg_exp).astype(BF16)
         grad_buf[...] = dot(d_neg_buf[...], neg_rows[...], ROW_COL)
@@ -405,7 +426,7 @@
 
 
 def adagrad(rows, state, grad, mean_of, learn_rate):
-    square = grad[0] * grad[0] + grad[1] * grad[1] + grad[2] * grad[2] + grad[3] * grad[3]
+    square = sum(g * g for g in grad)
     state = state + row_sum(square) / mean_of
     root = jnp.sqrt(state + EPSILON)
     return [r - learn_rate * (g / root) for r, g in zip(rows, grad)], state
@@ -513,7 +534,8 @@
             gs.append(start(remote(own.at[chunks + k], from_group.at[k], group_send.at[k], group_recv.at[k], grad_to)))
 
     def cross_copy(k):
-        return remote(send_buf.at[k], ent_wire.at[slot_of(bot, core, k)], out_send.at[2 * chunks + k], out_recv.at[slot_of(bot, core, k)], other_core)
+        slot = slot_of(bot, core, k)
+        return remote(send_buf.at[k], ent_wire.at[slot], out_send.at[2 * chunks + k], out_recv.at[slot], other_core)
 
     turn = (y + 4 - 2 * core) % 4
     near = 1 - turn % 2
@@ -581,12 +603,12 @@
         outs[k].wait_recv()
         store_table(turned(nxt), core, k)
         forwards.append(forward(1, turned(nxt), k, other_y))
-        crosses.append(forward(2, turned(nxt), k, other_core))
+        crosses.append((forward(2, turned(nxt), k, other_core), turned(nxt), k))
 
     def stage_cross(k):
         forwards[k].wait_recv()
         store_table(1 - turned(nxt), core, k)
-        crosses.append(forward(3, 1 - turned(nxt), k, other_core))
+        crosses.append((forward(3, 1 - turned(nxt), k, other_core), 1 - turned(nxt), k))
 
     stages = (stage_group, stage_update, stage_relay) if last else (stage_group, stage_update, stage_forward, stage_cross)
     rel_steps = len(rel_peers) - 1
@@ -620,11 +642,9 @@
             for k in range(chunks):
                 cross_copy(k).wait_send()
     else:
-        for n, copy in enumerate(crosses):
+        for copy, low, k in crosses:
             copy.wait_recv()
-        for low in CORES:
-            for k in range(chunks):
-                store_table(low, 1 - core, k)
+            store_table(low, 1 - core, k)
         for copy in stores:
             copy.wait()
     for copy in pending:
@@ -685,7 +705,7 @@
     shard = chunks // 4
 
     def load(n):
-        return pltpu.make_async_copy(ent_hbm.at[:, pl.ds(pl.multiple_of(n * chunk, chunk), chunk)], rows_buf.at[n % 4], load_sem.at[n % 4])
+        return pltpu.make_async_copy(ent_hbm.at[:, pl.ds(pl.multiple_of(n * chunk, chunk), chunk)], rows_buf.at[n % rows_buf.shape[0]], load_sem.at[n % rows_buf.shape[0]])
 
     def table_copy(q):
         part = table.at[pl.ds(q * shard, shard)]
@@ -699,34 +719,39 @@
         pltpu.make_async_copy(packed, shares.at[y], recv_sem.at[y]).start()
         neg_copy.start()
         neg_out[...] = neg_buf[...]
-        for n in range(3):
+        for n in range(AHEAD):
             load(n).start()
         for q in TILES:
-            def one(k, carry):
-                n = q * shard + k
-
-                @pl.when(n + 3 < chunks)
-                def _():
-                    load(n + 3).start()
-
-                load(n).wait()
-                tiles = columns_to_tiles(rows_buf[n % 4])
-                for t in TILES[:-1]:
-                    table[n, band(t, chunk), :] = tiles[t].astype(BF16)
-                table[n, 3 * chunk:, :] = fold_last(tiles[3]).astype(BF16)
-                place = pl.ds(pl.multiple_of(k * chunk * 4, chunk * 4), chunk * 4)
-
-                @pl.when(2 * bot + core == q)
-                def _():
-                    ent_out[place, :] = stack_tiles(tiles)
-
-                @pl.when(2 * bot + 1 - core == q)
-                def _():
-                    away[place, :] = stack_tiles(tiles)
+            def one(pair, carry):
+                first = 2 * pair
+                for c in CORES:
+                    n = q * shard + first + c
+
+                    @pl.when(n + AHEAD < chunks)
+                    def _():
+                        load(n + AHEAD).start()
+
+                    load(n).wait()
+                both = [(first + c, columns_to_tiles(rows_buf[(q * shard + first + c) % rows_buf.shape[0]])) for c in CORES]
+                for k, tiles in both:
+                    n = q * shard + k
+                    for t in TILES[:-1]:
+                        table[n, band(t, chunk), :] = tiles[t].astype(BF16)
+                    table[n, 3 * chunk:, :] = fold_last(tiles[3]).astype(BF16)
+                    rows = stack_tiles(tiles)
+                    place = pl.ds(pl.multiple_of(k * chunk * 4, chunk * 4), chunk * 4)
+
+                    @pl.when(2 * bot + core == q)
+                    def _():
+                        ent_out[place, :] = rows
+
+                    @pl.when(2 * bot + 1 - core == q)
+                    def _():
+                        away[place, :] = rows
 
                 return carry
 
-            lax.fori_loop(0, shard, one, 0)
+            lax.fori_loop(0, shard // 2, one, 0)
             table_copy(q).start()
 
             @pl.when(2 * bot + 1 - core == q)
@@ -790,7 +815,7 @@
         in_specs=[*[vmem] * 5, hbm, vmem],
         out_specs=(vmem,) * 7,
         scratch_shapes=[pltpu.VMEM(head.shape, jnp.int32), pltpu.VMEM((reps, *head.shape), jnp.int32), pltpu.VMEM((groups, 1, neg.shape[1]), jnp.int32),
-                        pltpu.VMEM((4, width, CHUNK), F32), pltpu.VMEM((rows, LANES), F32), *[dma_sems(4)] * 2, *[dma_sems(2)] * 2, *[dma_sems(4)] * 3],
+                        pltpu.VMEM((AHEAD + 2, width, CHUNK), F32), pltpu.VMEM((rows, LANES), F32), *[dma_sems(4)] * 2, *[dma_sems(2)] * 2, dma_sems(AHEAD + 2), *[dma_sems(4)] * 2],
         compiler_params=pltpu.CompilerParams(collective_id=20, has_side_effects=True),
         name='setup',
     )(head, tail, rel_ids, mask, neg, ent, rel)
@@ -803,7 +828,7 @@
         tiles.append(below(unfold_last(wire_ref[n, 3 * chunk:wire_rows(chunk), :])))
         ent_out[:, band(n, chunk)] = tiles_to_columns(tiles)
         state = below([part[:, :1] for part in unfold_last(wire_ref[n, wire_rows(chunk):, :])])
-        state_out[:, band(n, chunk)] = jnp.broadcast_to(state, (chunk, LANES)).T[:1]
+        state_out[:, band(n, chunk)] = column_sum(jnp.where(on_diagonal(chunk), state, 0.0))
 
     @pl.when(pl.program_id(0) == 0)
     def _():

time: 1010 us -> 999 us (0.989)
  Pallas kernels: 988 us -> 973 us
  transfers between devices with their start and end apart: 1 -> 1, of which waited for: 0 -> 0; matrix products, arithmetic and copies ran while one was open for 0% -> 0% of each run, Pallas kernels for 6% -> 5%
where the time goes in v1:
time: 999 us; the launch traced here: 983 us
  Pallas kernels  973 us (97%)
    pallas_call x8, Pallas kernels, exchange_call(): pl.pallas_call(functools.partial(exchange_kernel, (step, groups, chunks,...  739 us
    pallas_call x8, Pallas kernels, bucket_call(): pl.pallas_call(functools.partial(bucket_kernel, (step, tail_bits)), out_s...  201 us
    pallas_call x1, Pallas kernels, setup_call(): pl.pallas_call(functools.partial(setup_kernel, cfg), out_shape=(*(jax.Sha...  22.8 us
  transfers between devices with their start and end apart: 1, of which 0 were waited for; matrix products, arithmetic and copies ran while one was open for 0% of the time, Pallas kernels for 5%

profile of v1, /device:TPU:97, one launch (start us, length us, event | category | flops | bytes accessed | tf_op | source)
XLA Modules:
  0.0 983.1 jit_solution(9597320042881249859)
XLA Ops:
  0.7 0.7 dynamic_slice.10
  1.4 1.3 collective-permute-start
  2.7 1.6 pad.4.rel_ref
  4.3 22.8 %setup.1 = (s32[8,1,8704]{2,1,0:T(1,128)}, s32[8,1,8192]{2,1,0:T(1,128)}, s32[8,128]{1,0:T(8,128)}, s32[8,1,1024]{2,1,0:T(1,128)}, bf16[32,400,128]{2,1,0:T(8,12...) custom-call(s32[8,2048]{1,0:T(8,128)} %bitcast.31, s32[8,2048]{1,0:T(8,128)} %bitcast.32, s32[8,2048]{1,0:T(8,128)} %bitcast.33, ...), custom_call_target="tpu_custom_call" | custom-call | tf_op jit(solution)/shard_map/setup/pallas_call | solution.py:811
  27.1 28.9 %bucket.8 = (f32[32,400,128]{2,1,0:T(8,128)}, f32[8,400,128]{2,1,0:T(8,128)}, f32[400,128]{1,0:T(8,128)}) custom-call(s32[8,1,8704]{2,1,0:T(1,128)} %get-tuple-element.83.edges_hbm, s32[8,128]{1,0:T(8,128)} %get-tuple-element.84.count_ref, s32[8,1,1024]{2,1,0:T(1,128)} %get-tuple-element.85.negs_hbm, s32[8,1,8192]{2,1,0:T(1,128)} %get-tuple-element.86.rel_ids_hbm, ...), custom_call_target="tpu_custom_call" | custom-call | tf_op jit(solution)/shard_map/bucket/pallas_call | solution.py:393
  56.0 0.0 collective-permute-done
  56.0 0.7 dynamic-slice_select_fusion
  56.7 1.0 copy.12.state_ref
  57.7 0.6 broadcast_in_dim.7.rel_state_ref
  58.4 74.6 %exchange.8 = (f32[4096,128]{1,0:T(8,128)}, f32[1024,1]{1,0:T(8,128)}, f32[128,512]{1,0:T(8,128)}, f32[128,1]{1,0:T(8,128)}, f32[1,128]{1,0:T(1,128)}, /*index=5*/bf16[32,400,128]{2,1,0:T(8,128)(2,1)}) custom-call(f32[32,400,128]{2,1,0:T(8,128)} %get-tuple-element.90.tail_ref, f32[8,400,128]{2,1,0:T(8,128)} %get-tuple-element.91.head_hbm, ...), custom_call_target="tpu_custom_call" | custom-call | tf_op jit(solution)/shard_map/exchange/pallas_call | solution.py:666
  132.9 25.8 %bucket.9 = (f32[32,400,128]{2,1,0:T(8,128)}, f32[8,400,128]{2,1,0:T(8,128)}, f32[400,128]{1,0:T(8,128)}) custom-call(s32[8,1,8704]{2,1,0:T(1,128)} %get-tuple-element.83.edges_hbm, s32[8,128]{1,0:T(8,128)} %get-tuple-element.84.count_ref, s32[8,1,1024]{2,1,0:T(1,128)} %get-tuple-element.85.negs_hbm, s32[8,1,8192]{2,1,0:T(1,128)} %get-tuple-element.86.rel_ids_hbm, ...), custom_call_target="tpu_custom_call" | custom-call | tf_op jit(solution)/shard_map/bucket/pallas_call | solution.py:393
  158.7 74.4 %exchange.9 = (f32[4096,128]{1,0:T(8,128)}, f32[1024,1]{1,0:T(8,128)}, f32[128,512]{1,0:T(8,128)}, f32[128,1]{1,0:T(8,128)}, f32[1,128]{1,0:T(1,128)}, /*index=5*/bf16[32,400,128]{2,1,0:T(8,128)(2,1)}) custom-call(f32[32,400,128]{2,1,0:T(8,128)} %get-tuple-element.96.tail_ref, f32[8,400,128]{2,1,0:T(8,128)} %get-tuple-element.97.head_hbm, ...), custom_call_target="tpu_custom_call" | custom-call | tf_op jit(solution)/shard_map/exchange/pallas_call | solution.py:666
  233.1 31.1 %bucket.10 = (f32[32,400,128]{2,1,0:T(8,128)}, f32[8,400,128]{2,1,0:T(8,128)}, f32[400,128]{1,0:T(8,128)}) custom-call(s32[8,1,8704]{2,1,0:T(1,128)} %get-tuple-element.83.edges_hbm, s32[8,128]{1,0:T(8,128)} %get-tuple-element.84.count_ref, s32[8,1,1024]{2,1,0:T(1,128)} %get-tuple-element.85.negs_hbm, s32[8,1,8192]{2,1,0:T(1,128)} %get-tuple-element.86.rel_ids_hbm, ...), custom_call_target="tpu_custom_call" | custom-call | tf_op jit(solution)/shard_map/bucket/pallas_call | solution.py:393
  264.1 92.7 %exchange.10 = (f32[4096,128]{1,0:T(8,128)}, f32[1024,1]{1,0:T(8,128)}, f32[128,512]{1,0:T(8,128)}, f32[128,1]{1,0:T(8,128)}, f32[1,128]{1,0:T(1,128)}, /*index=5*/bf16[32,400,128]{2,1,0:T(8,128)(2,1)}) custom-call(f32[32,400,128]{2,1,0:T(8,128)} %get-tuple-element.104.tail_ref, f32[8,400,128]{2,1,0:T(8,128)} %get-tuple-element.105.head_hbm, ...), custom_call_target="tpu_custom_call" | custom-call | tf_op jit(solution)/shard_map/exchange/pallas_call | solution.py:666
  356.8 25.8 %bucket.11 = (f32[32,400,128]{2,1,0:T(8,128)}, f32[8,400,128]{2,1,0:T(8,128)}, f32[400,128]{1,0:T(8,128)}) custom-call(s32[8,1,8704]{2,1,0:T(1,128)} %get-tuple-element.83.edges_hbm, s32[8,128]{1,0:T(8,128)} %get-tuple-element.84.count_ref, s32[8,1,1024]{2,1,0:T(1,128)} %get-tuple-element.85.negs_hbm, s32[8,1,8192]{2,1,0:T(1,128)} %get-tuple-element.86.rel_ids_hbm, ...), custom_call_target="tpu_custom_call" | custom-call | tf_op jit(solution)/shard_map/bucket/pallas_call | solution.py:393
  382.7 96.3 %exchange.11 = (f32[4096,128]{1,0:T(8,128)}, f32[1024,1]{1,0:T(8,128)}, f32[128,512]{1,0:T(8,128)}, f32[128,1]{1,0:T(8,128)}, f32[1,128]{1,0:T(1,128)}, /*index=5*/bf16[32,400,128]{2,1,0:T(8,128)(2,1)}) custom-call(f32[32,400,128]{2,1,0:T(8,128)} %get-tuple-element.112.tail_ref, f32[8,400,128]{2,1,0:T(8,128)} %get-tuple-element.113.head_hbm, ...), custom_call_target="tpu_custom_call" | custom-call | tf_op jit(solution)/shard_map/exchange/pallas_call | solution.py:666
  479.0 17.5 %bucket.12 = (f32[32,400,128]{2,1,0:T(8,128)}, f32[8,400,128]{2,1,0:T(8,128)}, f32[400,128]{1,0:T(8,128)}) custom-call(s32[8,1,8704]{2,1,0:T(1,128)} %get-tuple-element.83.edges_hbm, s32[8,128]{1,0:T(8,128)} %get-tuple-element.84.count_ref, s32[8,1,1024]{2,1,0:T(1,128)} %get-tuple-element.85.negs_hbm, s32[8,1,8192]{2,1,0:T(1,128)} %get-tuple-element.86.rel_ids_hbm, ...), custom_call_target="tpu_custom_call" | custom-call | tf_op jit(solution)/shard_map/bucket/pallas_call | solution.py:393
  496.5 107.8 %exchange.12 = (f32[4096,128]{1,0:T(8,128)}, f32[1024,1]{1,0:T(8,128)}, f32[128,512]{1,0:T(8,128)}, f32[128,1]{1,0:T(8,128)}, f32[1,128]{1,0:T(1,128)}, /*index=5*/bf16[32,400,128]{2,1,0:T(8,128)(2,1)}) custom-call(f32[32,400,128]{2,1,0:T(8,128)} %get-tuple-element.120.tail_ref, f32[8,400,128]{2,1,0:T(8,128)} %get-tuple-element.121.head_hbm, ...), custom_call_target="tpu_custom_call" | custom-call | tf_op jit(solution)/shard_map/exchange/pallas_call | solution.py:666
  604.3 25.7 %bucket.13 = (f32[32,400,128]{2,1,0:T(8,128)}, f32[8,400,128]{2,1,0:T(8,128)}, f32[400,128]{1,0:T(8,128)}) custom-call(s32[8,1,8704]{2,1,0:T(1,128)} %get-tuple-element.83.edges_hbm, s32[8,128]{1,0:T(8,128)} %get-tuple-element.84.count_ref, s32[8,1,1024]{2,1,0:T(1,128)} %get-tuple-element.85.negs_hbm, s32[8,1,8192]{2,1,0:T(1,128)} %get-tuple-element.86.rel_ids_hbm, ...), custom_call_target="tpu_custom_call" | custom-call | tf_op jit(solution)/shard_map/bucket/pallas_call | solution.py:393
  630.1 90.1 %exchange.13 = (f32[4096,128]{1,0:T(8,128)}, f32[1024,1]{1,0:T(8,128)}, f32[128,512]{1,0:T(8,128)}, f32[128,1]{1,0:T(8,128)}, f32[1,128]{1,0:T(1,128)}, /*index=5*/bf16[32,400,128]{2,1,0:T(8,128)(2,1)}) custom-call(f32[32,400,128]{2,1,0:T(8,128)} %get-tuple-element.128.tail_ref, f32[8,400,128]{2,1,0:T(8,128)} %get-tuple-element.129.head_hbm, ...), custom_call_target="tpu_custom_call" | custom-call | tf_op jit(solution)/shard_map/exchange/pallas_call | solution.py:666
  720.2 28.5 %bucket.14 = (f32[32,400,128]{2,1,0:T(8,128)}, f32[8,400,128]{2,1,0:T(8,128)}, f32[400,128]{1,0:T(8,128)}) custom-call(s32[8,1,8704]{2,1,0:T(1,128)} %get-tuple-element.83.edges_hbm, s32[8,128]{1,0:T(8,128)} %get-tuple-element.84.count_ref, s32[8,1,1024]{2,1,0:T(1,128)} %get-tuple-element.85.negs_hbm, s32[8,1,8192]{2,1,0:T(1,128)} %get-tuple-element.86.rel_ids_hbm, ...), custom_call_target="tpu_custom_call" | custom-call | tf_op jit(solution)/shard_map/bucket/pallas_call | solution.py:393
  748.7 79.1 %exchange.14 = (f32[4096,128]{1,0:T(8,128)}, f32[1024,1]{1,0:T(8,128)}, f32[128,512]{1,0:T(8,128)}, f32[128,1]{1,0:T(8,128)}, f32[1,128]{1,0:T(1,128)}, /*index=5*/bf16[32,400,128]{2,1,0:T(8,128)(2,1)}) custom-call(f32[32,400,128]{2,1,0:T(8,128)} %get-tuple-element.136.tail_ref, f32[8,400,128]{2,1,0:T(8,128)} %get-tuple-element.137.head_hbm, ...), custom_call_target="tpu_custom_call" | custom-call | tf_op jit(solution)/shard_map/exchange/pallas_call | solution.py:666
  827.8 17.8 %bucket.15 = (f32[32,400,128]{2,1,0:T(8,128)}, f32[8,400,128]{2,1,0:T(8,128)}, f32[400,128]{1,0:T(8,128)}) custom-call(s32[8,1,8704]{2,1,0:T(1,128)} %get-tuple-element.83.edges_hbm, s32[8,128]{1,0:T(8,128)} %get-tuple-element.84.count_ref, s32[8,1,1024]{2,1,0:T(1,128)} %get-tuple-element.85.negs_hbm, s32[8,1,8192]{2,1,0:T(1,128)} %get-tuple-element.86.rel_ids_hbm, ...), custom_call_target="tpu_custom_call" | custom-call | tf_op jit(solution)/shard_map/bucket/pallas_call | solution.py:393
  845.6 0.0 copy-start
  845.6 0.0 copy-start.1
  845.6 0.0 copy-start.2
  845.6 0.0 copy-start.3
  845.7 123.6 %exchange.15 = (f32[32,416,128]{2,1,0:T(8,128)}, f32[128,512]{1,0:T(8,128)}, f32[1,128]{1,0:T(1,128)}) custom-call(f32[32,400,128]{2,1,0:T(8,128)} %get-tuple-element.144.tail_ref, f32[8,400,128]{2,1,0:T(8,128)} %get-tuple-element.145.head_hbm, f32[2,200,128]{2,1,0:T(8,128)} %bitcast.23, f32[4096,128]{1,0:T(8,128)} %get-tuple-element.141.ent_hbm, ...), custom_call_target="tpu_custom_call" | custom-call | tf_op jit(solution)/shard_map/exchange/pallas_call | solution.py:666
  969.4 0.6 concatenate.3
  970.0 10.2 %finish.1 = (f32[400,4096]{1,0:T(8,128)}, f32[1,4096]{1,0:T(1,128)}, f32[400,128]{1,0:T(8,128)}) custom-call(f32[32,416,128]{2,1,0:T(8,128)} %get-tuple-element.149.wire_ref, f32[128,512]{1,0:T(8,128)} %get-tuple-element.150.rel_ref), custom_call_target="tpu_custom_call" | custom-call | tf_op jit(solution)/shard_map/finish/pallas_call | solution.py:842
  980.3 1.6 slice_bitcast_fusion
  981.9 0.7 dynamic-slice_reduce_fusion
  (11 shorter events, 0.0 us)
Async XLA Ops:
  1.4 54.7 %collective-permute-start = (f32[1024]{0:T(1024)S(1)}, f32[1024]{0:T(1024)S(1)}, u32[]{:S(2)}, u32[]{:S(2)}) collective-permute-start(f32[1024]{0:T(1024)S(1)} %dynamic_slice.10), channel_id=1, source_target_pairs={{0,1},{2,3},{4,5},{6,7},{8,9},{10,11},{12,13},{14,15},{17,16},{19,... | collective-permute-start | bytes 12296 | tf_op jit(solution)/shard_map/ppermute | solution.py:874
  845.6 123.7 %copy-start = (f32[1,128]{1,0:T(1,128)S(1)}, f32[1,128]{1,0:T(1,128)}, u32[]{:S(2)}) copy-start(f32[1,128]{1,0:T(1,128)} %get-tuple-element.154) | copy-start | bytes 1540
  845.6 123.7 %copy-start.1 = (f32[1,128]{1,0:T(1,128)S(1)}, f32[1,128]{1,0:T(1,128)}, u32[]{:S(2)}) copy-start(f32[1,128]{1,0:T(1,128)} %get-tuple-element.155) | copy-start | bytes 1540
  845.6 123.7 %copy-start.2 = (f32[1,128]{1,0:T(1,128)S(1)}, f32[1,128]{1,0:T(1,128)}, u32[]{:S(2)}) copy-start(f32[1,128]{1,0:T(1,128)} %get-tuple-element.156) | copy-start | bytes 1540
  845.6 123.7 %copy-start.3 = (f32[1,128]{1,0:T(1,128)S(1)}, f32[1,128]{1,0:T(1,128)}, u32[]{:S(2)}) copy-start(f32[1,128]{1,0:T(1,128)} %get-tuple-element.157) | copy-start | bytes 1540
  845.6 123.7 %copy-start.4 = (f32[1,128]{1,0:T(1,128)S(1)}, f32[1,128]{1,0:T(1,128)}, u32[]{:S(2)}) copy-start(f32[1,128]{1,0:T(1,128)} %get-tuple-element.158) | copy-start | bytes 1540
  845.6 123.7 %copy-start.5 = (f32[1,128]{1,0:T(1,128)S(1)}, f32[1,128]{1,0:T(1,128)}, u32[]{:S(2)}) copy-start(f32[1,128]{1,0:T(1,128)} %get-tuple-element.159) | copy-start | bytes 1540
  845.7 123.7 %copy-start.6 = (f32[1,128]{1,0:T(1,128)S(1)}, f32[1,128]{1,0:T(1,128)}, u32[]{:S(2)}) copy-start(f32[1,128]{1,0:T(1,128)} %get-tuple-element.160) | copy-start | bytes 1540

commit v2 on v1

--- a/solution.py
+++ b/solution.py
@@ -18,7 +18,8 @@
 ROLLED = 32
 TOGETHER = 8
 AHEAD = 6
-LAG = 3
+LAGS = (0, 3, 6, 9)
+FAR_LAGS = (0, 5, 7, 9)
 PARTS = 4
 REL_HOPS = 6
 STRIP = 32
@@ -612,10 +613,12 @@
 
     stages = (stage_group, stage_update, stage_relay) if last else (stage_group, stage_update, stage_forward, stage_cross)
     rel_steps = len(rel_peers) - 1
-    for tick in range(chunks + LAG * (len(stages) - 1)):
-        for n, stage in enumerate(stages):
-            if 0 <= tick - LAG * n < chunks:
-                stage(tick - LAG * n)
+    far = groups <= 4 * step < 3 * groups
+    lags = FAR_LAGS if far else LAGS
+    for tick in range(chunks + lags[len(stages) - 1]):
+        for lag, stage in zip(lags, stages):
+            if 0 <= tick - lag < chunks:
+                stage(tick - lag)
         if tick % 2 == 1 and tick < 2 * rel_steps - 1:
             rel_step(tick // 2 + 1)
 
@@ -688,6 +691,7 @@
     head_bits, tail_bits, spare = cfg
     y, x, core, top, bot = where_here()
     home = core == top
+    own_shard, other_shard = 2 * bot + core, 2 * bot + 1 - core
     other_core = {'data': y, 'ent': 2 * x + 1 - core}
     users = [(c, 2 * core + d) for c in CORES for d in CORES]
     users = [({'data': row, 'ent': 2 * x + c}, (core == c) & (y == row)) for c, row in users]
@@ -741,11 +745,11 @@
                     rows = stack_tiles(tiles)
                     place = pl.ds(pl.multiple_of(k * chunk * 4, chunk * 4), chunk * 4)
 
-                    @pl.when(2 * bot + core == q)
+                    @pl.when(own_shard == q)
                     def _():
                         ent_out[place, :] = rows
 
-                    @pl.when(2 * bot + 1 - core == q)
+                    @pl.when(other_shard == q)
                     def _():
                         away[place, :] = rows
 
@@ -754,7 +758,7 @@
             lax.fori_loop(0, shard // 2, one, 0)
             table_copy(q).start()
 
-            @pl.when(2 * bot + 1 - core == q)
+            @pl.when(other_shard == q)
             def _():
                 ent_copy.start()
 
@@ -763,7 +767,7 @@
     for row in TILES:
         remote(packed, shares.at[row], send_sem.at[0], recv_sem.at[row], other_core).wait_recv()
     share = beside([shares[row] for row in TILES])
-    mine = ((share >> head_bits) & 3 == 2 * bot + core) & (share >> (2 * tail_bits) != spare)
+    mine = ((share >> head_bits) & 3 == own_shard) & (share >> (2 * tail_bits) != spare)
     lane = lanes(share.shape)
     width = share.shape[1]
     steps = (width - 1).bit_length()

time: 999 us -> 1000 us (level)
    pallas_call x8, Pallas kernels: 201 us -> 231 us  [bucket_call(): pl.pallas_call(functools.partial(bucket_kernel, (step, tail_bits)), out_s...]
    pallas_call x8, Pallas kernels: 739 us -> 709 us  [exchange_call(): pl.pallas_call(functools.partial(exchange_kernel, (step, groups, chunks,...]
  transfers between devices with their start and end apart: 1 -> 1, of which waited for: 0 -> 0; matrix products, arithmetic and copies ran while one was open for 0% -> 0% of each run, Pallas kernels for 5% -> 6%
where the time goes in v2:
time: 1000 us; the launch traced here: 983 us
  Pallas kernels  973 us (97%)
    pallas_call x8, Pallas kernels, exchange_call(): pl.pallas_call(functools.partial(exchange_kernel, (step, groups, chunks,...  709 us
    pallas_call x8, Pallas kernels, bucket_call(): pl.pallas_call(functools.partial(bucket_kernel, (step, tail_bits)), out_s...  231 us
    pallas_call x1, Pallas kernels, setup_call(): pl.pallas_call(functools.partial(setup_kernel, cfg), out_shape=(*(jax.Sha...  22.8 us
  transfers between devices with their start and end apart: 1, of which 0 were waited for; matrix products, arithmetic and copies ran while one was open for 0% of the time, Pallas kernels for 6%

profile of v2, /device:TPU:97, one launch (start us, length us, event | category | flops | bytes accessed | tf_op | source)
XLA Modules:
  0.0 983.5 jit_solution(5245288257418524217)
XLA Ops:
  0.7 0.7 dynamic_slice.10
  1.4 1.3 collective-permute-start
  2.7 1.6 pad.4.rel_ref
  4.3 22.8 %setup.1 = (s32[8,1,8704]{2,1,0:T(1,128)}, s32[8,1,8192]{2,1,0:T(1,128)}, s32[8,128]{1,0:T(8,128)}, s32[8,1,1024]{2,1,0:T(1,128)}, bf16[32,400,128]{2,1,0:T(8,12...) custom-call(s32[8,2048]{1,0:T(8,128)} %bitcast.31, s32[8,2048]{1,0:T(8,128)} %bitcast.32, s32[8,2048]{1,0:T(8,128)} %bitcast.33, ...), custom_call_target="tpu_custom_call" | custom-call | tf_op jit(solution)/shard_map/setup/pallas_call | solution.py:815
  27.1 37.0 %bucket.8 = (f32[32,400,128]{2,1,0:T(8,128)}, f32[8,400,128]{2,1,0:T(8,128)}, f32[400,128]{1,0:T(8,128)}) custom-call(s32[8,1,8704]{2,1,0:T(1,128)} %get-tuple-element.83.edges_hbm, s32[8,128]{1,0:T(8,128)} %get-tuple-element.84.count_ref, s32[8,1,1024]{2,1,0:T(1,128)} %get-tuple-element.85.negs_hbm, s32[8,1,8192]{2,1,0:T(1,128)} %get-tuple-element.86.rel_ids_hbm, ...), custom_call_target="tpu_custom_call" | custom-call | tf_op jit(solution)/shard_map/bucket/pallas_call | solution.py:394
  64.0 0.0 collective-permute-done
  64.1 0.7 dynamic-slice_select_fusion
  64.8 1.0 copy.12.state_ref
  65.8 0.6 broadcast_in_dim.7.rel_state_ref
  66.4 70.4 %exchange.8 = (f32[4096,128]{1,0:T(8,128)}, f32[1024,1]{1,0:T(8,128)}, f32[128,512]{1,0:T(8,128)}, f32[128,1]{1,0:T(8,128)}, f32[1,128]{1,0:T(1,128)}, /*index=5*/bf16[32,400,128]{2,1,0:T(8,128)(2,1)}) custom-call(f32[32,400,128]{2,1,0:T(8,128)} %get-tuple-element.90.tail_ref, f32[8,400,128]{2,1,0:T(8,128)} %get-tuple-element.91.head_hbm, ...), custom_call_target="tpu_custom_call" | custom-call | tf_op jit(solution)/shard_map/exchange/pallas_call | solution.py:669
  136.8 31.0 %bucket.9 = (f32[32,400,128]{2,1,0:T(8,128)}, f32[8,400,128]{2,1,0:T(8,128)}, f32[400,128]{1,0:T(8,128)}) custom-call(s32[8,1,8704]{2,1,0:T(1,128)} %get-tuple-element.83.edges_hbm, s32[8,128]{1,0:T(8,128)} %get-tuple-element.84.count_ref, s32[8,1,1024]{2,1,0:T(1,128)} %get-tuple-element.85.negs_hbm, s32[8,1,8192]{2,1,0:T(1,128)} %get-tuple-element.86.rel_ids_hbm, ...), custom_call_target="tpu_custom_call" | custom-call | tf_op jit(solution)/shard_map/bucket/pallas_call | solution.py:394
  167.8 72.2 %exchange.9 = (f32[4096,128]{1,0:T(8,128)}, f32[1024,1]{1,0:T(8,128)}, f32[128,512]{1,0:T(8,128)}, f32[128,1]{1,0:T(8,128)}, f32[1,128]{1,0:T(1,128)}, /*index=5*/bf16[32,400,128]{2,1,0:T(8,128)(2,1)}) custom-call(f32[32,400,128]{2,1,0:T(8,128)} %get-tuple-element.96.tail_ref, f32[8,400,128]{2,1,0:T(8,128)} %get-tuple-element.97.head_hbm, ...), custom_call_target="tpu_custom_call" | custom-call | tf_op jit(solution)/shard_map/exchange/pallas_call | solution.py:669
  240.0 17.7 %bucket.10 = (f32[32,400,128]{2,1,0:T(8,128)}, f32[8,400,128]{2,1,0:T(8,128)}, f32[400,128]{1,0:T(8,128)}) custom-call(s32[8,1,8704]{2,1,0:T(1,128)} %get-tuple-element.83.edges_hbm, s32[8,128]{1,0:T(8,128)} %get-tuple-element.84.count_ref, s32[8,1,1024]{2,1,0:T(1,128)} %get-tuple-element.85.negs_hbm, s32[8,1,8192]{2,1,0:T(1,128)} %get-tuple-element.86.rel_ids_hbm, ...), custom_call_target="tpu_custom_call" | custom-call | tf_op jit(solution)/shard_map/bucket/pallas_call | solution.py:394
  257.8 103.6 %exchange.10 = (f32[4096,128]{1,0:T(8,128)}, f32[1024,1]{1,0:T(8,128)}, f32[128,512]{1,0:T(8,128)}, f32[128,1]{1,0:T(8,128)}, f32[1,128]{1,0:T(1,128)}, /*index=5*/bf16[32,400,128]{2,1,0:T(8,128)(2,1)}) custom-call(f32[32,400,128]{2,1,0:T(8,128)} %get-tuple-element.104.tail_ref, f32[8,400,128]{2,1,0:T(8,128)} %get-tuple-element.105.head_hbm, ...), custom_call_target="tpu_custom_call" | custom-call | tf_op jit(solution)/shard_map/exchange/pallas_call | solution.py:669
  361.4 25.8 %bucket.11 = (f32[32,400,128]{2,1,0:T(8,128)}, f32[8,400,128]{2,1,0:T(8,128)}, f32[400,128]{1,0:T(8,128)}) custom-call(s32[8,1,8704]{2,1,0:T(1,128)} %get-tuple-element.83.edges_hbm, s32[8,128]{1,0:T(8,128)} %get-tuple-element.84.count_ref, s32[8,1,1024]{2,1,0:T(1,128)} %get-tuple-element.85.negs_hbm, s32[8,1,8192]{2,1,0:T(1,128)} %get-tuple-element.86.rel_ids_hbm, ...), custom_call_target="tpu_custom_call" | custom-call | tf_op jit(solution)/shard_map/bucket/pallas_call | solution.py:394
  387.2 82.2 %exchange.11 = (f32[4096,128]{1,0:T(8,128)}, f32[1024,1]{1,0:T(8,128)}, f32[128,512]{1,0:T(8,128)}, f32[128,1]{1,0:T(8,128)}, f32[1,128]{1,0:T(1,128)}, /*index=5*/bf16[32,400,128]{2,1,0:T(8,128)(2,1)}) custom-call(f32[32,400,128]{2,1,0:T(8,128)} %get-tuple-element.112.tail_ref, f32[8,400,128]{2,1,0:T(8,128)} %get-tuple-element.113.head_hbm, ...), custom_call_target="tpu_custom_call" | custom-call | tf_op jit(solution)/shard_map/exchange/pallas_call | solution.py:669
  469.4 25.7 %bucket.12 = (f32[32,400,128]{2,1,0:T(8,128)}, f32[8,400,128]{2,1,0:T(8,128)}, f32[400,128]{1,0:T(8,128)}) custom-call(s32[8,1,8704]{2,1,0:T(1,128)} %get-tuple-element.83.edges_hbm, s32[8,128]{1,0:T(8,128)} %get-tuple-element.84.count_ref, s32[8,1,1024]{2,1,0:T(1,128)} %get-tuple-element.85.negs_hbm, s32[8,1,8192]{2,1,0:T(1,128)} %get-tuple-element.86.rel_ids_hbm, ...), custom_call_target="tpu_custom_call" | custom-call | tf_op jit(solution)/shard_map/bucket/pallas_call | solution.py:394
  495.2 101.0 %exchange.12 = (f32[4096,128]{1,0:T(8,128)}, f32[1024,1]{1,0:T(8,128)}, f32[128,512]{1,0:T(8,128)}, f32[128,1]{1,0:T(8,128)}, f32[1,128]{1,0:T(1,128)}, /*index=5*/bf16[32,400,128]{2,1,0:T(8,128)(2,1)}) custom-call(f32[32,400,128]{2,1,0:T(8,128)} %get-tuple-element.120.tail_ref, f32[8,400,128]{2,1,0:T(8,128)} %get-tuple-element.121.head_hbm, ...), custom_call_target="tpu_custom_call" | custom-call | tf_op jit(solution)/shard_map/exchange/pallas_call | solution.py:669
  596.2 23.1 %bucket.13 = (f32[32,400,128]{2,1,0:T(8,128)}, f32[8,400,128]{2,1,0:T(8,128)}, f32[400,128]{1,0:T(8,128)}) custom-call(s32[8,1,8704]{2,1,0:T(1,128)} %get-tuple-element.83.edges_hbm, s32[8,128]{1,0:T(8,128)} %get-tuple-element.84.count_ref, s32[8,1,1024]{2,1,0:T(1,128)} %get-tuple-element.85.negs_hbm, s32[8,1,8192]{2,1,0:T(1,128)} %get-tuple-element.86.rel_ids_hbm, ...), custom_call_target="tpu_custom_call" | custom-call | tf_op jit(solution)/shard_map/bucket/pallas_call | solution.py:394
  619.3 97.6 %exchange.13 = (f32[4096,128]{1,0:T(8,128)}, f32[1024,1]{1,0:T(8,128)}, f32[128,512]{1,0:T(8,128)}, f32[128,1]{1,0:T(8,128)}, f32[1,128]{1,0:T(1,128)}, /*index=5*/bf16[32,400,128]{2,1,0:T(8,128)(2,1)}) custom-call(f32[32,400,128]{2,1,0:T(8,128)} %get-tuple-element.128.tail_ref, f32[8,400,128]{2,1,0:T(8,128)} %get-tuple-element.129.head_hbm, ...), custom_call_target="tpu_custom_call" | custom-call | tf_op jit(solution)/shard_map/exchange/pallas_call | solution.py:669
  716.9 36.7 %bucket.14 = (f32[32,400,128]{2,1,0:T(8,128)}, f32[8,400,128]{2,1,0:T(8,128)}, f32[400,128]{1,0:T(8,128)}) custom-call(s32[8,1,8704]{2,1,0:T(1,128)} %get-tuple-element.83.edges_hbm, s32[8,128]{1,0:T(8,128)} %get-tuple-element.84.count_ref, s32[8,1,1024]{2,1,0:T(1,128)} %get-tuple-element.85.negs_hbm, s32[8,1,8192]{2,1,0:T(1,128)} %get-tuple-element.86.rel_ids_hbm, ...), custom_call_target="tpu_custom_call" | custom-call | tf_op jit(solution)/shard_map/bucket/pallas_call | solution.py:394
  753.6 68.0 %exchange.14 = (f32[4096,128]{1,0:T(8,128)}, f32[1024,1]{1,0:T(8,128)}, f32[128,512]{1,0:T(8,128)}, f32[128,1]{1,0:T(8,128)}, f32[1,128]{1,0:T(1,128)}, /*index=5*/bf16[32,400,128]{2,1,0:T(8,128)(2,1)}) custom-call(f32[32,400,128]{2,1,0:T(8,128)} %get-tuple-element.136.tail_ref, f32[8,400,128]{2,1,0:T(8,128)} %get-tuple-element.137.head_hbm, ...), custom_call_target="tpu_custom_call" | custom-call | tf_op jit(solution)/shard_map/exchange/pallas_call | solution.py:669
  821.6 33.9 %bucket.15 = (f32[32,400,128]{2,1,0:T(8,128)}, f32[8,400,128]{2,1,0:T(8,128)}, f32[400,128]{1,0:T(8,128)}) custom-call(s32[8,1,8704]{2,1,0:T(1,128)} %get-tuple-element.83.edges_hbm, s32[8,128]{1,0:T(8,128)} %get-tuple-element.84.count_ref, s32[8,1,1024]{2,1,0:T(1,128)} %get-tuple-element.85.negs_hbm, s32[8,1,8192]{2,1,0:T(1,128)} %get-tuple-element.86.rel_ids_hbm, ...), custom_call_target="tpu_custom_call" | custom-call | tf_op jit(solution)/shard_map/bucket/pallas_call | solution.py:394
  855.6 0.0 copy-start
  855.6 0.0 copy-start.1
  855.6 0.0 copy-start.2
  855.6 0.0 copy-start.3
  855.6 114.1 %exchange.15 = (f32[32,416,128]{2,1,0:T(8,128)}, f32[128,512]{1,0:T(8,128)}, f32[1,128]{1,0:T(1,128)}) custom-call(f32[32,400,128]{2,1,0:T(8,128)} %get-tuple-element.144.tail_ref, f32[8,400,128]{2,1,0:T(8,128)} %get-tuple-element.145.head_hbm, f32[2,200,128]{2,1,0:T(8,128)} %bitcast.23, f32[4096,128]{1,0:T(8,128)} %get-tuple-element.141.ent_hbm, ...), custom_call_target="tpu_custom_call" | custom-call | tf_op jit(solution)/shard_map/exchange/pallas_call | solution.py:669
  969.8 0.6 concatenate.3
  970.4 10.2 %finish.1 = (f32[400,4096]{1,0:T(8,128)}, f32[1,4096]{1,0:T(1,128)}, f32[400,128]{1,0:T(8,128)}) custom-call(f32[32,416,128]{2,1,0:T(8,128)} %get-tuple-element.149.wire_ref, f32[128,512]{1,0:T(8,128)} %get-tuple-element.150.rel_ref), custom_call_target="tpu_custom_call" | custom-call | tf_op jit(solution)/shard_map/finish/pallas_call | solution.py:846
  980.7 1.6 slice_bitcast_fusion
  982.3 0.7 dynamic-slice_reduce_fusion
  (11 shorter events, 0.0 us)
Async XLA Ops:
  1.4 62.7 %collective-permute-start = (f32[1024]{0:T(1024)S(1)}, f32[1024]{0:T(1024)S(1)}, u32[]{:S(2)}, u32[]{:S(2)}) collective-permute-start(f32[1024]{0:T(1024)S(1)} %dynamic_slice.10), channel_id=1, source_target_pairs={{0,1},{2,3},{4,5},{6,7},{8,9},{10,11},{12,13},{14,15},{17,16},{19,... | collective-permute-start | bytes 12296 | tf_op jit(solution)/shard_map/ppermute | solution.py:878
  855.6 114.2 %copy-start = (f32[1,128]{1,0:T(1,128)S(1)}, f32[1,128]{1,0:T(1,128)}, u32[]{:S(2)}) copy-start(f32[1,128]{1,0:T(1,128)} %get-tuple-element.154) | copy-start | bytes 1540
  855.6 114.2 %copy-start.1 = (f32[1,128]{1,0:T(1,128)S(1)}, f32[1,128]{1,0:T(1,128)}, u32[]{:S(2)}) copy-start(f32[1,128]{1,0:T(1,128)} %get-tuple-element.155) | copy-start | bytes 1540
  855.6 114.2 %copy-start.2 = (f32[1,128]{1,0:T(1,128)S(1)}, f32[1,128]{1,0:T(1,128)}, u32[]{:S(2)}) copy-start(f32[1,128]{1,0:T(1,128)} %get-tuple-element.156) | copy-start | bytes 1540
  855.6 114.2 %copy-start.3 = (f32[1,128]{1,0:T(1,128)S(1)}, f32[1,128]{1,0:T(1,128)}, u32[]{:S(2)}) copy-start(f32[1,128]{1,0:T(1,128)} %get-tuple-element.157) | copy-start | bytes 1540
  855.6 114.2 %copy-start.4 = (f32[1,128]{1,0:T(1,128)S(1)}, f32[1,128]{1,0:T(1,128)}, u32[]{:S(2)}) copy-start(f32[1,128]{1,0:T(1,128)} %get-tuple-element.158) | copy-start | bytes 1540
  855.6 114.2 %copy-start.5 = (f32[1,128]{1,0:T(1,128)S(1)}, f32[1,128]{1,0:T(1,128)}, u32[]{:S(2)}) copy-start(f32[1,128]{1,0:T(1,128)} %get-tuple-element.159) | copy-start | bytes 1540
  855.6 114.2 %copy-start.6 = (f32[1,128]{1,0:T(1,128)S(1)}, f32[1,128]{1,0:T(1,128)}, u32[]{:S(2)}) copy-start(f32[1,128]{1,0:T(1,128)} %get-tuple-element.160) | copy-start | bytes 1540

commit v3 on v2

--- a/solution.py
+++ b/solution.py
@@ -615,12 +615,13 @@
     rel_steps = len(rel_peers) - 1
     far = groups <= 4 * step < 3 * groups
     lags = FAR_LAGS if far else LAGS
+    rel_ticks = (1, 3, chunks, chunks + 3)
     for tick in range(chunks + lags[len(stages) - 1]):
         for lag, stage in zip(lags, stages):
             if 0 <= tick - lag < chunks:
                 stage(tick - lag)
-        if tick % 2 == 1 and tick < 2 * rel_steps - 1:
-            rel_step(tick // 2 + 1)
+        if tick in rel_ticks:
+            rel_step(rel_ticks.index(tick) + 1)
 
     rel_copies[rel_steps].wait_recv()
     halves = rel_sum[rel_steps - 1], rel_from[rel_steps]

time: 1000 us -> 1000 us (level)
  the two profiles are of different devices: /device:TPU:97 before, /device:TPU:107 now
where the time goes in v3:
time: 1000 us; the launch traced here: 1010 us
  Pallas kernels  1000 us (100%)
    pallas_call x8, Pallas kernels, exchange_call(): pl.pallas_call(functools.partial(exchange_kernel, (step, groups, chunks,...  721 us
    pallas_call x8, Pallas kernels, bucket_call(): pl.pallas_call(functools.partial(bucket_kernel, (step, tail_bits)), out_s...  248 us
    pallas_call x1, Pallas kernels, setup_call(): pl.pallas_call(functools.partial(setup_kernel, cfg), out_shape=(*(jax.Sha...  22.5 us
  transfers between devices with their start and end apart: 1, of which 0 were waited for; matrix products, arithmetic and copies ran while one was open for 0% of the time, Pallas kernels for 6%

profile of v3, /device:TPU:107, one launch (start us, length us, event | category | flops | bytes accessed | tf_op | source)
XLA Modules:
  0.0 1011.6 jit_solution(16753541163096475129)
XLA Ops:
  0.7 0.7 dynamic_slice.10
  1.4 1.3 collective-permute-start
  2.7 1.6 pad.4.rel_ref
  4.3 22.5 %setup.1 = (s32[8,1,8704]{2,1,0:T(1,128)}, s32[8,1,8192]{2,1,0:T(1,128)}, s32[8,128]{1,0:T(8,128)}, s32[8,1,1024]{2,1,0:T(1,128)}, bf16[32,400,128]{2,1,0:T(8,12...) custom-call(s32[8,2048]{1,0:T(8,128)} %bitcast.31, s32[8,2048]{1,0:T(8,128)} %bitcast.32, s32[8,2048]{1,0:T(8,128)} %bitcast.33, ...), custom_call_target="tpu_custom_call" | custom-call | tf_op jit(solution)/shard_map/setup/pallas_call | solution.py:816
  26.8 34.3 %bucket.8 = (f32[32,400,128]{2,1,0:T(8,128)}, f32[8,400,128]{2,1,0:T(8,128)}, f32[400,128]{1,0:T(8,128)}) custom-call(s32[8,1,8704]{2,1,0:T(1,128)} %get-tuple-element.83.edges_hbm, s32[8,128]{1,0:T(8,128)} %get-tuple-element.84.count_ref, s32[8,1,1024]{2,1,0:T(1,128)} %get-tuple-element.85.negs_hbm, s32[8,1,8192]{2,1,0:T(1,128)} %get-tuple-element.86.rel_ids_hbm, ...), custom_call_target="tpu_custom_call" | custom-call | tf_op jit(solution)/shard_map/bucket/pallas_call | solution.py:394
  61.1 0.0 collective-permute-done
  61.1 0.7 dynamic-slice_select_fusion
  61.8 1.0 copy.12.state_ref
  62.8 0.6 broadcast_in_dim.7.rel_state_ref
  63.5 70.0 %exchange.8 = (f32[4096,128]{1,0:T(8,128)}, f32[1024,1]{1,0:T(8,128)}, f32[128,512]{1,0:T(8,128)}, f32[128,1]{1,0:T(8,128)}, f32[1,128]{1,0:T(1,128)}, /*index=5*/bf16[32,400,128]{2,1,0:T(8,128)(2,1)}) custom-call(f32[32,400,128]{2,1,0:T(8,128)} %get-tuple-element.90.tail_ref, f32[8,400,128]{2,1,0:T(8,128)} %get-tuple-element.91.head_hbm, ...), custom_call_target="tpu_custom_call" | custom-call | tf_op jit(solution)/shard_map/exchange/pallas_call | solution.py:670
  133.4 39.5 %bucket.9 = (f32[32,400,128]{2,1,0:T(8,128)}, f32[8,400,128]{2,1,0:T(8,128)}, f32[400,128]{1,0:T(8,128)}) custom-call(s32[8,1,8704]{2,1,0:T(1,128)} %get-tuple-element.83.edges_hbm, s32[8,128]{1,0:T(8,128)} %get-tuple-element.84.count_ref, s32[8,1,1024]{2,1,0:T(1,128)} %get-tuple-element.85.negs_hbm, s32[8,1,8192]{2,1,0:T(1,128)} %get-tuple-element.86.rel_ids_hbm, ...), custom_call_target="tpu_custom_call" | custom-call | tf_op jit(solution)/shard_map/bucket/pallas_call | solution.py:394
  173.0 69.2 %exchange.9 = (f32[4096,128]{1,0:T(8,128)}, f32[1024,1]{1,0:T(8,128)}, f32[128,512]{1,0:T(8,128)}, f32[128,1]{1,0:T(8,128)}, f32[1,128]{1,0:T(1,128)}, /*index=5*/bf16[32,400,128]{2,1,0:T(8,128)(2,1)}) custom-call(f32[32,400,128]{2,1,0:T(8,128)} %get-tuple-element.96.tail_ref, f32[8,400,128]{2,1,0:T(8,128)} %get-tuple-element.97.head_hbm, ...), custom_call_target="tpu_custom_call" | custom-call | tf_op jit(solution)/shard_map/exchange/pallas_call | solution.py:670
  242.1 36.6 %bucket.10 = (f32[32,400,128]{2,1,0:T(8,128)}, f32[8,400,128]{2,1,0:T(8,128)}, f32[400,128]{1,0:T(8,128)}) custom-call(s32[8,1,8704]{2,1,0:T(1,128)} %get-tuple-element.83.edges_hbm, s32[8,128]{1,0:T(8,128)} %get-tuple-element.84.count_ref, s32[8,1,1024]{2,1,0:T(1,128)} %get-tuple-element.85.negs_hbm, s32[8,1,8192]{2,1,0:T(1,128)} %get-tuple-element.86.rel_ids_hbm, ...), custom_call_target="tpu_custom_call" | custom-call | tf_op jit(solution)/shard_map/bucket/pallas_call | solution.py:394
  278.7 92.9 %exchange.10 = (f32[4096,128]{1,0:T(8,128)}, f32[1024,1]{1,0:T(8,128)}, f32[128,512]{1,0:T(8,128)}, f32[128,1]{1,0:T(8,128)}, f32[1,128]{1,0:T(1,128)}, /*index=5*/bf16[32,400,128]{2,1,0:T(8,128)(2,1)}) custom-call(f32[32,400,128]{2,1,0:T(8,128)} %get-tuple-element.104.tail_ref, f32[8,400,128]{2,1,0:T(8,128)} %get-tuple-element.105.head_hbm, ...), custom_call_target="tpu_custom_call" | custom-call | tf_op jit(solution)/shard_map/exchange/pallas_call | solution.py:670
  371.6 23.2 %bucket.11 = (f32[32,400,128]{2,1,0:T(8,128)}, f32[8,400,128]{2,1,0:T(8,128)}, f32[400,128]{1,0:T(8,128)}) custom-call(s32[8,1,8704]{2,1,0:T(1,128)} %get-tuple-element.83.edges_hbm, s32[8,128]{1,0:T(8,128)} %get-tuple-element.84.count_ref, s32[8,1,1024]{2,1,0:T(1,128)} %get-tuple-element.85.negs_hbm, s32[8,1,8192]{2,1,0:T(1,128)} %get-tuple-element.86.rel_ids_hbm, ...), custom_call_target="tpu_custom_call" | custom-call | tf_op jit(solution)/shard_map/bucket/pallas_call | solution.py:394
  394.8 89.9 %exchange.11 = (f32[4096,128]{1,0:T(8,128)}, f32[1024,1]{1,0:T(8,128)}, f32[128,512]{1,0:T(8,128)}, f32[128,1]{1,0:T(8,128)}, f32[1,128]{1,0:T(1,128)}, /*index=5*/bf16[32,400,128]{2,1,0:T(8,128)(2,1)}) custom-call(f32[32,400,128]{2,1,0:T(8,128)} %get-tuple-element.112.tail_ref, f32[8,400,128]{2,1,0:T(8,128)} %get-tuple-element.113.head_hbm, ...), custom_call_target="tpu_custom_call" | custom-call | tf_op jit(solution)/shard_map/exchange/pallas_call | solution.py:670
  484.8 36.7 %bucket.12 = (f32[32,400,128]{2,1,0:T(8,128)}, f32[8,400,128]{2,1,0:T(8,128)}, f32[400,128]{1,0:T(8,128)}) custom-call(s32[8,1,8704]{2,1,0:T(1,128)} %get-tuple-element.83.edges_hbm, s32[8,128]{1,0:T(8,128)} %get-tuple-element.84.count_ref, s32[8,1,1024]{2,1,0:T(1,128)} %get-tuple-element.85.negs_hbm, s32[8,1,8192]{2,1,0:T(1,128)} %get-tuple-element.86.rel_ids_hbm, ...), custom_call_target="tpu_custom_call" | custom-call | tf_op jit(solution)/shard_map/bucket/pallas_call | solution.py:394
  521.5 98.9 %exchange.12 = (f32[4096,128]{1,0:T(8,128)}, f32[1024,1]{1,0:T(8,128)}, f32[128,512]{1,0:T(8,128)}, f32[128,1]{1,0:T(8,128)}, f32[1,128]{1,0:T(1,128)}, /*index=5*/bf16[32,400,128]{2,1,0:T(8,128)(2,1)}) custom-call(f32[32,400,128]{2,1,0:T(8,128)} %get-tuple-element.120.tail_ref, f32[8,400,128]{2,1,0:T(8,128)} %get-tuple-element.121.head_hbm, ...), custom_call_target="tpu_custom_call" | custom-call | tf_op jit(solution)/shard_map/exchange/pallas_call | solution.py:670
  620.4 23.2 %bucket.13 = (f32[32,400,128]{2,1,0:T(8,128)}, f32[8,400,128]{2,1,0:T(8,128)}, f32[400,128]{1,0:T(8,128)}) custom-call(s32[8,1,8704]{2,1,0:T(1,128)} %get-tuple-element.83.edges_hbm, s32[8,128]{1,0:T(8,128)} %get-tuple-element.84.count_ref, s32[8,1,1024]{2,1,0:T(1,128)} %get-tuple-element.85.negs_hbm, s32[8,1,8192]{2,1,0:T(1,128)} %get-tuple-element.86.rel_ids_hbm, ...), custom_call_target="tpu_custom_call" | custom-call | tf_op jit(solution)/shard_map/bucket/pallas_call | solution.py:394
  643.6 96.8 %exchange.13 = (f32[4096,128]{1,0:T(8,128)}, f32[1024,1]{1,0:T(8,128)}, f32[128,512]{1,0:T(8,128)}, f32[128,1]{1,0:T(8,128)}, f32[1,128]{1,0:T(1,128)}, /*index=5*/bf16[32,400,128]{2,1,0:T(8,128)(2,1)}) custom-call(f32[32,400,128]{2,1,0:T(8,128)} %get-tuple-element.128.tail_ref, f32[8,400,128]{2,1,0:T(8,128)} %get-tuple-element.129.head_hbm, ...), custom_call_target="tpu_custom_call" | custom-call | tf_op jit(solution)/shard_map/exchange/pallas_call | solution.py:670
  740.5 17.7 %bucket.14 = (f32[32,400,128]{2,1,0:T(8,128)}, f32[8,400,128]{2,1,0:T(8,128)}, f32[400,128]{1,0:T(8,128)}) custom-call(s32[8,1,8704]{2,1,0:T(1,128)} %get-tuple-element.83.edges_hbm, s32[8,128]{1,0:T(8,128)} %get-tuple-element.84.count_ref, s32[8,1,1024]{2,1,0:T(1,128)} %get-tuple-element.85.negs_hbm, s32[8,1,8192]{2,1,0:T(1,128)} %get-tuple-element.86.rel_ids_hbm, ...), custom_call_target="tpu_custom_call" | custom-call | tf_op jit(solution)/shard_map/bucket/pallas_call | solution.py:394
  758.2 91.9 %exchange.14 = (f32[4096,128]{1,0:T(8,128)}, f32[1024,1]{1,0:T(8,128)}, f32[128,512]{1,0:T(8,128)}, f32[128,1]{1,0:T(8,128)}, f32[1,128]{1,0:T(1,128)}, /*index=5*/bf16[32,400,128]{2,1,0:T(8,128)(2,1)}) custom-call(f32[32,400,128]{2,1,0:T(8,128)} %get-tuple-element.136.tail_ref, f32[8,400,128]{2,1,0:T(8,128)} %get-tuple-element.137.head_hbm, ...), custom_call_target="tpu_custom_call" | custom-call | tf_op jit(solution)/shard_map/exchange/pallas_call | solution.py:670
  850.1 36.5 %bucket.15 = (f32[32,400,128]{2,1,0:T(8,128)}, f32[8,400,128]{2,1,0:T(8,128)}, f32[400,128]{1,0:T(8,128)}) custom-call(s32[8,1,8704]{2,1,0:T(1,128)} %get-tuple-element.83.edges_hbm, s32[8,128]{1,0:T(8,128)} %get-tuple-element.84.count_ref, s32[8,1,1024]{2,1,0:T(1,128)} %get-tuple-element.85.negs_hbm, s32[8,1,8192]{2,1,0:T(1,128)} %get-tuple-element.86.rel_ids_hbm, ...), custom_call_target="tpu_custom_call" | custom-call | tf_op jit(solution)/shard_map/bucket/pallas_call | solution.py:394
  886.6 0.0 copy-start
  886.6 0.0 copy-start.1
  886.6 0.0 copy-start.2
  886.7 0.0 copy-start.3
  886.7 111.1 %exchange.15 = (f32[32,416,128]{2,1,0:T(8,128)}, f32[128,512]{1,0:T(8,128)}, f32[1,128]{1,0:T(1,128)}) custom-call(f32[32,400,128]{2,1,0:T(8,128)} %get-tuple-element.144.tail_ref, f32[8,400,128]{2,1,0:T(8,128)} %get-tuple-element.145.head_hbm, f32[2,200,128]{2,1,0:T(8,128)} %bitcast.23, f32[4096,128]{1,0:T(8,128)} %get-tuple-element.141.ent_hbm, ...), custom_call_target="tpu_custom_call" | custom-call | tf_op jit(solution)/shard_map/exchange/pallas_call | solution.py:670
  997.9 0.6 concatenate.3
  998.5 10.2 %finish.1 = (f32[400,4096]{1,0:T(8,128)}, f32[1,4096]{1,0:T(1,128)}, f32[400,128]{1,0:T(8,128)}) custom-call(f32[32,416,128]{2,1,0:T(8,128)} %get-tuple-element.149.wire_ref, f32[128,512]{1,0:T(8,128)} %get-tuple-element.150.rel_ref), custom_call_target="tpu_custom_call" | custom-call | tf_op jit(solution)/shard_map/finish/pallas_call | solution.py:847
  1008.8 1.6 slice_bitcast_fusion
  1010.4 0.7 dynamic-slice_reduce_fusion
  (11 shorter events, 0.0 us)
Async XLA Ops:
  1.4 59.8 %collective-permute-start = (f32[1024]{0:T(1024)S(1)}, f32[1024]{0:T(1024)S(1)}, u32[]{:S(2)}, u32[]{:S(2)}) collective-permute-start(f32[1024]{0:T(1024)S(1)} %dynamic_slice.10), channel_id=1, source_target_pairs={{0,1},{2,3},{4,5},{6,7},{8,9},{10,11},{12,13},{14,15},{17,16},{19,... | collective-permute-start | bytes 12296 | tf_op jit(solution)/shard_map/ppermute | solution.py:879
  886.6 111.2 %copy-start = (f32[1,128]{1,0:T(1,128)S(1)}, f32[1,128]{1,0:T(1,128)}, u32[]{:S(2)}) copy-start(f32[1,128]{1,0:T(1,128)} %get-tuple-element.154) | copy-start | bytes 1540
  886.6 111.2 %copy-start.1 = (f32[1,128]{1,0:T(1,128)S(1)}, f32[1,128]{1,0:T(1,128)}, u32[]{:S(2)}) copy-start(f32[1,128]{1,0:T(1,128)} %get-tuple-element.155) | copy-start | bytes 1540
  886.6 111.2 %copy-start.2 = (f32[1,128]{1,0:T(1,128)S(1)}, f32[1,128]{1,0:T(1,128)}, u32[]{:S(2)}) copy-start(f32[1,128]{1,0:T(1,128)} %get-tuple-element.156) | copy-start | bytes 1540
  886.7 111.2 %copy-start.3 = (f32[1,128]{1,0:T(1,128)S(1)}, f32[1,128]{1,0:T(1,128)}, u32[]{:S(2)}) copy-start(f32[1,128]{1,0:T(1,128)} %get-tuple-element.157) | copy-start | bytes 1540
  886.7 111.2 %copy-start.4 = (f32[1,128]{1,0:T(1,128)S(1)}, f32[1,128]{1,0:T(1,128)}, u32[]{:S(2)}) copy-start(f32[1,128]{1,0:T(1,128)} %get-tuple-element.158) | copy-start | bytes 1540
  886.7 111.2 %copy-start.5 = (f32[1,128]{1,0:T(1,128)S(1)}, f32[1,128]{1,0:T(1,128)}, u32[]{:S(2)}) copy-start(f32[1,128]{1,0:T(1,128)} %get-tuple-element.159) | copy-start | bytes 1540
  886.7 111.2 %copy-start.6 = (f32[1,128]{1,0:T(1,128)S(1)}, f32[1,128]{1,0:T(1,128)}, u32[]{:S(2)}) copy-start(f32[1,128]{1,0:T(1,128)} %get-tuple-element.160) | copy-start | bytes 1540
